TPU v7x, 8 devices: a whole 2x2x1 slice. The times are simulated.
8 devices in a mesh: data: 2 (over z, y), cp: 4 (over x, core).
Axes of the slice: x: 2, y: 2, z: 1, core: 2. Of those that a mesh axis runs over, the one named last changes fastest.
Arguments:
- x_tokens: bfloat16 [32, 1024, 1536], P('data', 'cp'), parts along dimension 0
- positions: int32 [32, 1024], P('data', 'cp'), parts along dimension 0
- w_query: bfloat16 [1536, 1536], replicated
- w_key: bfloat16 [1536, 256], replicated
- w_value: bfloat16 [1536, 256], replicated
- w_out: bfloat16 [1536, 1536], replicated
Outputs:
- output: bfloat16 [32, 1024, 1536], P('data', 'cp'), parts along dimension 0
There are 2 independent parts. A program takes and returns all parts, laid end to end along the dimension named above; an argument that names none is the same for every part.
All inputs are finite; a program needn't handle non-finite values.
Results may differ from a plain program's by a relative error of at most 0.00437571.
Values are sent between devices in bfloat16 or wider.
A program may use at most 1 GiB of HBM per device.

v0:
```python
import jax
import jax.numpy as jnp
from jax import lax
from jax.sharding import PartitionSpec as P

HEAD_DIM = 128
ROPE_BASE = 500000
MASK_FILL = -1e30


def apply_rope(head_vecs, positions):
    half_dim = HEAD_DIM // 2
    inv_freq = 1.0 / (ROPE_BASE ** (jnp.arange(0, HEAD_DIM, 2, dtype=jnp.float32) / HEAD_DIM))
    angles = positions.astype(jnp.float32)[:, :, None] * inv_freq
    tab_shape = angles.shape[:2] + (1,) * (head_vecs.ndim - 3) + (half_dim,)
    cosine = jnp.cos(angles).reshape(tab_shape)
    sine_tab = jnp.sin(angles).reshape(tab_shape)
    lower_half = head_vecs[..., :half_dim].astype(jnp.float32)
    upper_half = head_vecs[..., half_dim:].astype(jnp.float32)
    rotated = jnp.concatenate([lower_half * cosine - upper_half * sine_tab, upper_half * cosine + lower_half * sine_tab], axis=-1)
    return rotated.astype(jnp.bfloat16)


def project_qkv(x_rows, pos_rows, w_query, w_key, w_value):
    batch_rows, tok_rows, model_dim = x_rows.shape
    kv_heads = w_key.shape[1] // HEAD_DIM
    group_size = w_query.shape[1] // w_key.shape[1]
    flat_x = x_rows.reshape(batch_rows * tok_rows, model_dim)
    q_proj = jnp.dot(flat_x, w_query, preferred_element_type=jnp.float32).astype(jnp.bfloat16)
    k_proj = jnp.dot(flat_x, w_key, preferred_element_type=jnp.float32).astype(jnp.bfloat16)
    v_proj = jnp.dot(flat_x, w_value, preferred_element_type=jnp.float32).astype(jnp.bfloat16)
    q_rot = apply_rope(q_proj.reshape(batch_rows, tok_rows, kv_heads, group_size, HEAD_DIM), pos_rows)
    k_rot = apply_rope(k_proj.reshape(batch_rows, tok_rows, kv_heads, HEAD_DIM), pos_rows)
    return q_rot, k_rot, v_proj.reshape(batch_rows, tok_rows, kv_heads, HEAD_DIM)


def empty_state(q_rot):
    batch_rows, tok_rows, kv_heads, group_size, _ = q_rot.shape
    state_shape = (batch_rows, kv_heads, group_size, tok_rows)
    return (jnp.full(state_shape, MASK_FILL, jnp.float32), jnp.zeros(state_shape, jnp.float32), jnp.zeros(state_shape + (HEAD_DIM,), jnp.float32))


def attend_block(q_rows, k_blk, v_blk, carry_state, allowed):
    m_run, l_run, acc_run = carry_state
    scores = jnp.einsum('bqhgd,bkhd->bhgqk', q_rows, k_blk, preferred_element_type=jnp.float32) * (HEAD_DIM ** -0.5)
    if allowed is not None:
        scores = jnp.where(allowed, scores, MASK_FILL)
    m_new = jnp.maximum(m_run, jnp.max(scores, axis=-1))
    exp_w = jnp.exp(scores - m_new[..., None])
    if allowed is not None:
        exp_w = jnp.where(allowed, exp_w, 0.0)
    rescale = jnp.exp(m_run - m_new)
    l_new = rescale * l_run + jnp.sum(exp_w, axis=-1)
    pv_part = jnp.einsum('bhgqk,bkhd->bhgqd', exp_w.astype(jnp.bfloat16), v_blk, preferred_element_type=jnp.float32)
    return m_new, l_new, rescale[..., None] * acc_run + pv_part


def attend_remote(q_loc, k_recv, v_recv, carry_state, src_before):
    half_len = q_loc.shape[1] // 2

    def keys_before(state_in):
        return attend_block(q_loc, k_recv[:, :half_len], v_recv[:, :half_len], state_in, None)

    def keys_after(state_in):
        m_run, l_run, acc_run = state_in
        tail_state = (m_run[..., half_len:], l_run[..., half_len:], acc_run[..., half_len:, :])
        m_new, l_new, acc_new = attend_block(q_loc[:, half_len:], k_recv, v_recv, tail_state, None)
        return (jnp.concatenate([m_run[..., :half_len], m_new], axis=-1), jnp.concatenate([l_run[..., :half_len], l_new], axis=-1), jnp.concatenate([acc_run[..., :half_len, :], acc_new], axis=-2))

    return lax.cond(src_before, keys_before, keys_after, carry_state)


def output_proj(x_rows, final_state, w_out):
    _, l_run, acc_run = final_state
    kv_heads, group_size = acc_run.shape[1], acc_run.shape[2]
    normed = (acc_run / l_run[..., None]).astype(jnp.bfloat16)
    w_heads = w_out.reshape(kv_heads, group_size, HEAD_DIM, w_out.shape[1])
    out_proj = jnp.einsum('bhgqd,hgde->bqe', normed, w_heads, preferred_element_type=jnp.float32)
    return (x_rows.astype(jnp.float32) + out_proj).astype(jnp.bfloat16)


def solution(mesh):
    cp_size = mesh.shape['cp']
    row_spec = P('data', 'cp', None)
    pos_spec = P('data', 'cp')
    rep_spec = P(None, None)
    shift_pairs = [(src_dev, (src_dev + 1) % cp_size) for src_dev in range(cp_size)]

    def local_block(x_loc, pos_loc, w_query, w_key, w_value, w_out):
        my_idx = lax.axis_index('cp')
        q_loc, k_loc, v_loc = project_qkv(x_loc, pos_loc, w_query, w_key, w_value)
        allowed = (pos_loc[:, None, :] <= pos_loc[:, :, None])[:, None, None]
        diag_state = attend_block(q_loc, k_loc, v_loc, empty_state(q_loc), allowed)

        def shift_step(step_idx, loop_in):
            k_cur, v_cur, carry_state = loop_in
            k_next = lax.ppermute(k_cur, 'cp', shift_pairs)
            v_next = lax.ppermute(v_cur, 'cp', shift_pairs)
            src_idx = (my_idx - step_idx) % cp_size
            return k_next, v_next, attend_remote(q_loc, k_next, v_next, carry_state, src_idx < my_idx)

        _, _, final_state = lax.fori_loop(1, cp_size, shift_step, (k_loc, v_loc, diag_state))
        return output_proj(x_loc, final_state, w_out)

    return jax.shard_map(local_block, mesh=mesh, in_specs=(row_spec, pos_spec, rep_spec, rep_spec, rep_spec, rep_spec), out_specs=row_spec, check_vma=False)
```

profile of v0, /device:TPU:0, one launch (start us, length us, event | category | flops | bytes accessed | tf_op | source)
XLA Modules:
  0.0 639.8 jit_solution(10497829847507533643)
XLA Ops:
  0.0 25.9 %convolution_convert_fusion = bf16[4096,1536]{1,0:T(8,128)(2,1)} fusion(bf16[4096,1536]{1,0:T(8,128)(2,1)} %bitcast.97, bf16[1536,1536]{1,0:T(8,128)(2,1)} %param.12), kind=kOutput, calls=%fused_computation.59 | convolution fusion | flops 19333644288 | bytes 29884416 | tf_op jit(solution)/shard_map/dot_general | solution.py:29
  25.9 26.0 %reshape.60 = bf16[16,256,2,6,128]{4,3,2,1,0:T(8,128)(2,1)} reshape(bf16[4096,1536]{1,0:T(8,128)(2,1)} %convolution_convert_fusion) | data formatting | bytes 25165824 | tf_op jit(solution)/shard_map/reshape | solution.py:32
  52.0 21.0 %fusion.59 = (bf16[16,256,2,6,64]{4,3,2,1,0:T(8,128)(2,1)S(1)}, bf16[16,256,2,6,64]{4,3,2,1,0:T(8,128)(2,1)}) fusion(bf16[16,256,2,6,128]{4,3,2,1,0:T(8,128)(2,1)} %reshape.60), kind=kLoop, calls=%fused_computation.86 | loop fusion | bytes 25165824 | tf_op jit(solution)/shard_map/slice | solution.py:18
  81.8 15.7 %fusion.35 = (bf16[16,256,2,6,64]{4,1,3,2,0:T(8,128)(2,1)S(1)}, bf16[16,256,2,6,64]{4,1,3,2,0:T(8,128)(2,1)}) fusion(f32[16,256,64]{2,1,0:T(8,128)} %get-tuple-element.316, f32[16,256,64]{2,1,0:T(8,128)} %get-tuple-element.315, bf16[16,256,2,6,64]{4,3,2,1,0:T(8,128)(2,1)} %get-tuple-element.308, bf16[16,256,2,6,64]{4,3,2,1,0:T(8,128)(2,1)S(1)} %get-tuple-element.307), kind=kLoop, calls=%fused_computation.47 | loop fusion | flops 31457280 | bytes 27262976 | tf_op jit(solution)/shard_map/convert
  136.0 22.9 %fusion.31 = (f32[16,2,6,256]{3,2,1,0:T(8,128)S(1)}, f32[16,2,256,256,6]{3,2,4,1,0:T(8,128)}) fusion(pred[16,256,256]{1,2,0:T(8,128)(4,1)S(1)} %broadcast_compare_fusion, bf16[16,256,2,6,128]{4,1,3,2,0:T(8,128)(2,1)} %pad_maximum_fusion.3, bf16[16,256,2,128]{3,1,2,0:T(8,128)(2,1)} %pad_maximum_fusion.4), kind=kOutput, calls=%fused_computation.39 | convolution fusion | flops 3258925056 | bytes 66256896 | tf_op jit(solution)/shard_map/bqhgd,bkhd->bhgqk/dot_general | solution.py:45
  158.9 22.0 %fusion.33 = f32[16,2,6,256]{3,2,1,0:T(8,128)S(1)} fusion(f32[16,2,256,256,6]{3,2,4,1,0:T(8,128)} %get-tuple-element.318, f32[16,2,6,256]{3,2,1,0:T(8,128)S(1)} %broadcast_maximum_fusion, pred[16,256,256]{1,2,0:T(8,128)(4,1)S(1)} %broadcast_compare_fusion), kind=kLoop, calls=%fused_computation.41 | loop fusion | flops 62865408 | bytes 51773440 | tf_op jit(solution)/shard_map/reduce_sum | solution.py:53
  194.4 31.6 %broadcast_add_fusion = f32[16,2,6,256,128]{4,3,2,1,0:T(8,128)} fusion(f32[16,2,6,256]{3,2,1,0:T(8,128)S(1)} %get-tuple-element.313, f32[16,2,256,256,6]{3,2,4,1,0:T(8,128)} %get-tuple-element.318, f32[16,2,6,256]{3,2,1,0:T(8,128)S(1)} %broadcast_maximum_fusion, pred[16,256,256]{1,2,0:T(8,128)(4,1)S(1)} %broadcast_compare_fusion, ...), kind=kOutput, calls=%fused_computation.61 | convolution fusion | flops 3290431488 | bytes 79036416 | tf_op jit(solution)/shard_map/bhgqk,bkhd->bhgqd/dot_general | solution.py:54
  229.4 382.5 %while.23 = (s32[]{:T(128)}, bf16[16,256,2,128]{3,1,2,0:T(8,128)(2,1)}, bf16[16,256,2,128]{3,1,2,0:T(8,128)(2,1)}, f32[16,2,6,256]{3,2,1,0:T(8,128)S(1)}, f32[16...) while((s32[]{:T(128)}, ...), condition=%wide.region_9.10_spmd, body=%wide.region_2.9_spmd.sunk | while | flops 3284287488 | bytes 214761936 | solution.py:102
  233.2 23.0 %collective-permute-done = bf16[16,256,2,128]{3,1,2,0:T(8,128)(2,1)S(1)} collective-permute-done((bf16[16,256,2,128]{3,1,2,0:T(8,128)(2,1)}, bf16[16,256,2,128]{3,1,2,0:T(8,128)(2,1)S(1)}, u32[]{:S(2)}, u32[]{:S(2)}) %collective-permute-start) | collective-permute-done | bytes 2097184 | tf_op jit(solution)/shard_map/while/body/eval_jaxpr/ppermute | solution.py:97
  256.2 22.5 %collective-permute-done.1 = bf16[16,256,2,128]{3,1,2,0:T(8,128)(2,1)} collective-permute-done((bf16[16,256,2,128]{3,1,2,0:T(8,128)(2,1)}, bf16[16,256,2,128]{3,1,2,0:T(8,128)(2,1)}, u32[]{:S(2)}, u32[]{:S(2)}) %collective-permute-start.1) | collective-permute-done | bytes 2097184 | tf_op jit(solution)/shard_map/while/body/eval_jaxpr/ppermute | solution.py:98
  278.7 73.7 %conditional.2 = (f32[16,2,6,256]{3,2,1,0:T(8,128)}, f32[16,2,6,256]{3,2,1,0:T(8,128)S(1)}, f32[16,2,6,256,128]{4,3,2,1,0:T(8,128)}) conditional(s32[]{:T(128)} %convert_element_type.119, (f32[16,2,6,256]{3,2,1,0:T(8,128)S(1)}, bf16[16,256,2,6,128]{4,1,3,2,0:T(8,128)(2,1)}, bf16[16,256,2,128]{3,1,2,0:T(8,128)(2,1)S(1)}, ...), branch_computations={%region_3.5_spmd, %region_6.8_spmd} | conditional | flops 3284287488 | bytes 189202464 | solution.py:70
  302.3 20.6 %multiply_add_fusion = f32[16,2,6,128,128]{4,3,2,1,0:T(8,128)} fusion(f32[16,2,6,256,128]{4,3,2,1,0:T(8,128)} %get-tuple-element.237, f32[16,2,6,128]{3,2,1,0:T(8,128)S(1)} %get-tuple-element.294, bf16[16,256,2,128]{3,1,2,0:T(8,128)(2,1)} %get-tuple-element.238, f32[16,2,256,128,6]{3,2,4,1,0:T(8,128)} %get-tuple-element.300, ...), kind=kOutput, calls=%fused_computation.7 | convolution fusion | flops 1635778560 | bytes 52625408 | tf_op jit(solution)/shard_map/while/body/eval_jaxpr/cond/branch_0_fun/bhgqk,bkhd->bhgqd/dot_general | solution.py:54
  334.2 17.5 %pad_maximum_fusion = f32[16,2,6,256,128]{4,3,2,1,0:T(8,128)} fusion(f32[16,2,6,128,128]{4,3,2,1,0:T(8,128)} %multiply_add_fusion, f32[16,2,6,128,128]{4,3,2,1,0:T(8,128)} %slice.31), kind=kLoop, calls=%fused_computation | loop fusion | flops 6291456 | bytes 50331648 | tf_op jit(solution)/shard_map/while/body/eval_jaxpr/cond/branch_0_fun/concatenate | solution.py:68
  357.8 25.5 %collective-permute-done = bf16[16,256,2,128]{3,1,2,0:T(8,128)(2,1)S(1)} collective-permute-done((bf16[16,256,2,128]{3,1,2,0:T(8,128)(2,1)}, bf16[16,256,2,128]{3,1,2,0:T(8,128)(2,1)S(1)}, u32[]{:S(2)}, u32[]{:S(2)}) %collective-permute-start) | collective-permute-done | bytes 2097184 | tf_op jit(solution)/shard_map/while/body/eval_jaxpr/ppermute | solution.py:97
  383.3 22.5 %collective-permute-done.1 = bf16[16,256,2,128]{3,1,2,0:T(8,128)(2,1)} collective-permute-done((bf16[16,256,2,128]{3,1,2,0:T(8,128)(2,1)}, bf16[16,256,2,128]{3,1,2,0:T(8,128)(2,1)}, u32[]{:S(2)}, u32[]{:S(2)}) %collective-permute-start.1) | collective-permute-done | bytes 2097184 | tf_op jit(solution)/shard_map/while/body/eval_jaxpr/ppermute | solution.py:98
  405.7 73.7 %conditional.2 = (f32[16,2,6,256]{3,2,1,0:T(8,128)}, f32[16,2,6,256]{3,2,1,0:T(8,128)S(1)}, f32[16,2,6,256,128]{4,3,2,1,0:T(8,128)}) conditional(s32[]{:T(128)} %convert_element_type.119, (f32[16,2,6,256]{3,2,1,0:T(8,128)S(1)}, bf16[16,256,2,6,128]{4,1,3,2,0:T(8,128)(2,1)}, bf16[16,256,2,128]{3,1,2,0:T(8,128)(2,1)S(1)}, ...), branch_computations={%region_3.5_spmd, %region_6.8_spmd} | conditional | flops 3284287488 | bytes 189202464 | solution.py:70
  429.3 20.6 %multiply_add_fusion = f32[16,2,6,128,128]{4,3,2,1,0:T(8,128)} fusion(f32[16,2,6,256,128]{4,3,2,1,0:T(8,128)} %get-tuple-element.237, f32[16,2,6,128]{3,2,1,0:T(8,128)S(1)} %get-tuple-element.294, bf16[16,256,2,128]{3,1,2,0:T(8,128)(2,1)} %get-tuple-element.238, f32[16,2,256,128,6]{3,2,4,1,0:T(8,128)} %get-tuple-element.300, ...), kind=kOutput, calls=%fused_computation.7 | convolution fusion | flops 1635778560 | bytes 52625408 | tf_op jit(solution)/shard_map/while/body/eval_jaxpr/cond/branch_0_fun/bhgqk,bkhd->bhgqd/dot_general | solution.py:54
  461.2 17.5 %pad_maximum_fusion = f32[16,2,6,256,128]{4,3,2,1,0:T(8,128)} fusion(f32[16,2,6,128,128]{4,3,2,1,0:T(8,128)} %multiply_add_fusion, f32[16,2,6,128,128]{4,3,2,1,0:T(8,128)} %slice.31), kind=kLoop, calls=%fused_computation | loop fusion | flops 6291456 | bytes 50331648 | tf_op jit(solution)/shard_map/while/body/eval_jaxpr/cond/branch_0_fun/concatenate | solution.py:68
  484.8 25.5 %collective-permute-done = bf16[16,256,2,128]{3,1,2,0:T(8,128)(2,1)S(1)} collective-permute-done((bf16[16,256,2,128]{3,1,2,0:T(8,128)(2,1)}, bf16[16,256,2,128]{3,1,2,0:T(8,128)(2,1)S(1)}, u32[]{:S(2)}, u32[]{:S(2)}) %collective-permute-start) | collective-permute-done | bytes 2097184 | tf_op jit(solution)/shard_map/while/body/eval_jaxpr/ppermute | solution.py:97
  510.3 22.5 %collective-permute-done.1 = bf16[16,256,2,128]{3,1,2,0:T(8,128)(2,1)} collective-permute-done((bf16[16,256,2,128]{3,1,2,0:T(8,128)(2,1)}, bf16[16,256,2,128]{3,1,2,0:T(8,128)(2,1)}, u32[]{:S(2)}, u32[]{:S(2)}) %collective-permute-start.1) | collective-permute-done | bytes 2097184 | tf_op jit(solution)/shard_map/while/body/eval_jaxpr/ppermute | solution.py:98
  532.8 73.7 %conditional.2 = (f32[16,2,6,256]{3,2,1,0:T(8,128)}, f32[16,2,6,256]{3,2,1,0:T(8,128)S(1)}, f32[16,2,6,256,128]{4,3,2,1,0:T(8,128)}) conditional(s32[]{:T(128)} %convert_element_type.119, (f32[16,2,6,256]{3,2,1,0:T(8,128)S(1)}, bf16[16,256,2,6,128]{4,1,3,2,0:T(8,128)(2,1)}, bf16[16,256,2,128]{3,1,2,0:T(8,128)(2,1)S(1)}, ...), branch_computations={%region_3.5_spmd, %region_6.8_spmd} | conditional | flops 3284287488 | bytes 189202464 | solution.py:70
  556.4 20.6 %multiply_add_fusion = f32[16,2,6,128,128]{4,3,2,1,0:T(8,128)} fusion(f32[16,2,6,256,128]{4,3,2,1,0:T(8,128)} %get-tuple-element.237, f32[16,2,6,128]{3,2,1,0:T(8,128)S(1)} %get-tuple-element.294, bf16[16,256,2,128]{3,1,2,0:T(8,128)(2,1)} %get-tuple-element.238, f32[16,2,256,128,6]{3,2,4,1,0:T(8,128)} %get-tuple-element.300, ...), kind=kOutput, calls=%fused_computation.7 | convolution fusion | flops 1635778560 | bytes 52625408 | tf_op jit(solution)/shard_map/while/body/eval_jaxpr/cond/branch_0_fun/bhgqk,bkhd->bhgqd/dot_general | solution.py:54
  588.2 17.5 %pad_maximum_fusion = f32[16,2,6,256,128]{4,3,2,1,0:T(8,128)} fusion(f32[16,2,6,128,128]{4,3,2,1,0:T(8,128)} %multiply_add_fusion, f32[16,2,6,128,128]{4,3,2,1,0:T(8,128)} %slice.31), kind=kLoop, calls=%fused_computation | loop fusion | flops 6291456 | bytes 50331648 | tf_op jit(solution)/shard_map/while/body/eval_jaxpr/cond/branch_0_fun/concatenate | solution.py:68
  611.9 27.5 %fusion.40 = bf16[16,256,1536]{2,1,0:T(8,128)(2,1)} fusion(bf16[16,256,1536]{2,1,0:T(8,128)(2,1)} %param.10, bf16[2,6,128,1536,1]{3,2,1,0,4:T(8,128)(2,1)} %bitcast.100, f32[16,2,6,256,128]{4,3,2,1,0:T(8,128)} %get-tuple-element.259, f32[16,2,6,256]{3,2,1,0:T(8,128)S(1)} %get-tuple-element.260), kind=kOutput, calls=%fused_computation.52 | convolution fusion | flops 19358810112 | bytes 55246848 | tf_op jit(solution)/shard_map/bhgqd,hgde->bqe/dot_general | solution.py:78
  (58 shorter events, 190.8 us)
Async XLA Ops:
  0.0 111.0 %copy-start = (bf16[1536,256]{1,0:T(8,128)(2,1)S(1)}, bf16[1536,256]{1,0:T(8,128)(2,1)}, u32[]{:S(2)}) copy-start(bf16[1536,256]{1,0:T(8,128)(2,1)} %param.13) | copy-start | bytes 2359300
  52.0 21.0 %copy-start.3 = (s32[16,256]{1,0:T(8,128)S(1)}, s32[16,256]{1,0:T(8,128)}, u32[]{:S(2)}) copy-start(s32[16,256]{1,0:T(8,128)} %param.11) | copy-start | bytes 49156
  111.0 19.1 %copy-start.2 = (f32[16,256,64]{2,1,0:T(8,128)S(1)}, f32[16,256,64]{2,1,0:T(8,128)}, u32[]{:S(2)}) copy-start(f32[16,256,64]{2,1,0:T(8,128)} %get-tuple-element.315) | copy-start | bytes 3145732
  158.9 22.2 %copy-start.4 = (bf16[1536,256]{1,0:T(8,128)(2,1)S(1)}, bf16[1536,256]{1,0:T(8,128)(2,1)}, u32[]{:S(2)}) copy-start(bf16[1536,256]{1,0:T(8,128)(2,1)} %param.14) | copy-start | bytes 2359300
  229.7 26.5 %collective-permute-start = (bf16[16,256,2,128]{3,1,2,0:T(8,128)(2,1)}, bf16[16,256,2,128]{3,1,2,0:T(8,128)(2,1)S(1)}, u32[]{:S(2)}, u32[]{:S(2)}) collective-permute-start(bf16[16,256,2,128]{3,1,2,0:T(8,128)(2,1)} %get-tuple-element.393), channel_id=1, source_target_pairs={{0,1},{1,2},{2,3},{3,0},{4,5},{5,6},{6,7},{7,4}} | collective-permute-start | bytes 6291464 | tf_op jit(solution)/shard_map/while/body/eval_jaxpr/ppermute | solution.py:97
  230.6 48.1 %collective-permute-start.1 = (bf16[16,256,2,128]{3,1,2,0:T(8,128)(2,1)}, bf16[16,256,2,128]{3,1,2,0:T(8,128)(2,1)}, u32[]{:S(2)}, u32[]{:S(2)}) collective-permute-start(bf16[16,256,2,128]{3,1,2,0:T(8,128)(2,1)} %get-tuple-element.394), channel_id=1, source_target_pairs={{0,1},{1,2},{2,3},{3,0},{4,5},{5,6},{6,7},{7,4}} | collective-permute-start | bytes 6291464 | tf_op jit(solution)/shard_map/while/body/eval_jaxpr/ppermute | solution.py:98
  357.8 25.5 %collective-permute-start = (bf16[16,256,2,128]{3,1,2,0:T(8,128)(2,1)}, bf16[16,256,2,128]{3,1,2,0:T(8,128)(2,1)S(1)}, u32[]{:S(2)}, u32[]{:S(2)}) collective-permute-start(bf16[16,256,2,128]{3,1,2,0:T(8,128)(2,1)} %get-tuple-element.393), channel_id=1, source_target_pairs={{0,1},{1,2},{2,3},{3,0},{4,5},{5,6},{6,7},{7,4}} | collective-permute-start | bytes 6291464 | tf_op jit(solution)/shard_map/while/body/eval_jaxpr/ppermute | solution.py:97
  357.8 47.9 %collective-permute-start.1 = (bf16[16,256,2,128]{3,1,2,0:T(8,128)(2,1)}, bf16[16,256,2,128]{3,1,2,0:T(8,128)(2,1)}, u32[]{:S(2)}, u32[]{:S(2)}) collective-permute-start(bf16[16,256,2,128]{3,1,2,0:T(8,128)(2,1)} %get-tuple-element.394), channel_id=1, source_target_pairs={{0,1},{1,2},{2,3},{3,0},{4,5},{5,6},{6,7},{7,4}} | collective-permute-start | bytes 6291464 | tf_op jit(solution)/shard_map/while/body/eval_jaxpr/ppermute | solution.py:98
  484.8 25.5 %collective-permute-start = (bf16[16,256,2,128]{3,1,2,0:T(8,128)(2,1)}, bf16[16,256,2,128]{3,1,2,0:T(8,128)(2,1)S(1)}, u32[]{:S(2)}, u32[]{:S(2)}) collective-permute-start(bf16[16,256,2,128]{3,1,2,0:T(8,128)(2,1)} %get-tuple-element.393), channel_id=1, source_target_pairs={{0,1},{1,2},{2,3},{3,0},{4,5},{5,6},{6,7},{7,4}} | collective-permute-start | bytes 6291464 | tf_op jit(solution)/shard_map/while/body/eval_jaxpr/ppermute | solution.py:97
  484.8 47.9 %collective-permute-start.1 = (bf16[16,256,2,128]{3,1,2,0:T(8,128)(2,1)}, bf16[16,256,2,128]{3,1,2,0:T(8,128)(2,1)}, u32[]{:S(2)}, u32[]{:S(2)}) collective-permute-start(bf16[16,256,2,128]{3,1,2,0:T(8,128)(2,1)} %get-tuple-element.394), channel_id=1, source_target_pairs={{0,1},{1,2},{2,3},{3,0},{4,5},{5,6},{6,7},{7,4}} | collective-permute-start | bytes 6291464 | tf_op jit(solution)/shard_map/while/body/eval_jaxpr/ppermute | solution.py:98
  611.9 27.5 %copy-start.1 = (bf16[1536,256]{1,0:T(8,128)(2,1)S(1)}, bf16[1536,256]{1,0:T(8,128)(2,1)}, u32[]{:S(2)}) copy-start(bf16[1536,256]{1,0:T(8,128)(2,1)} %param.13) | copy-start | bytes 2359300
where the time goes:
time: 649 us; the launch traced here: 640 us
  matrix products  227 us (35%)
  other arithmetic  153 us (24%)
  waiting for transfers between devices  141 us (22%)
  local copies, waits for them, and re-layouts  114 us (18%)
    dot_general x4, matrix products, attend_block(): jnp.einsum('bhgqk,bkhd->bhgqd', exp_w.astype(jnp.bfloat16), v_blk, prefer...  93.4 us
    ppermute x3, waiting for transfers between devices, shift_step(): k_next = lax.ppermute(k_cur, 'cp', shift_pairs)  73.9 us
    ppermute x3, waiting for transfers between devices, shift_step(): v_next = lax.ppermute(v_cur, 'cp', shift_pairs)  67.4 us
    dot_general x4, matrix products, attend_block(): jnp.einsum('bqhgd,bkhd->bhgqk', q_rows, k_blk, preferred_element_type=jnp...  61.5 us
    reduce_sum x4, other arithmetic, attend_block(): l_new = rescale * l_run + jnp.sum(exp_w, axis=-1)  53.8 us
    concatenate x3, other arithmetic, keys_after(): jnp.concatenate([acc_run[..., :half_len, :], acc_new], axis=-2)  52.4 us
    slice x3, local copies, waits for them, and re-layouts, keys_after(): acc_run[..., :half_len, :]  34 us
    dot_general x1, matrix products, output_proj(): jnp.einsum('bhgqd,hgde->bqe', normed, w_heads, preferred_element_type=jnp...  27.5 us
  transfers between devices with their start and end apart: 6, of which 6 were waited for; matrix products, arithmetic and copies ran while one was open for 0% of the time, Pallas kernels for 0%

commit v1 on v0

v1 whole, which is shorter than its diff:
```python
import functools
import math

import jax
import jax.numpy as jnp
from jax import lax
from jax.experimental import pallas as pl
from jax.experimental.pallas import tpu as pltpu
from jax.sharding import PartitionSpec as P

HEAD_DIM = 128
HALF_DIM = HEAD_DIM // 2
ROPE_BASE = 500000
MASK_FILL = -1e30
EXP_SCALE = math.log2(math.e) * HEAD_DIM ** -0.5
CP_SIZE = 4
BLK = 128
MESH = pl.DeviceIdType.MESH


def nt_dot(lhs, rhs):
    return lax.dot_general(lhs, rhs, (((1,), (1,)), ((), ())), preferred_element_type=jnp.float32)


def rope_head(head, cos_tab, sin_tab):
    wide = head.astype(jnp.float32)
    return (wide * cos_tab + pltpu.roll(wide, HALF_DIM, 1) * sin_tab).astype(jnp.bfloat16)


def kernel(x_hbm, pos_ref, freq_ref, wq_hbm, wk_hbm, wv_hbm, wo_hbm, y_hbm,
           xb, wq, wk, wv, wo, kv, qb, ob, cos_b, sin_b,
           xsem, wsem, ysem, ici_s, ici_r, sib_s, sib_r, fwd_s, fwd_r):
    rows, toks, width = xb.shape
    kv_cols = wk.shape[1]
    kv_heads = kv_cols // HEAD_DIM
    q_heads = wq.shape[1] // HEAD_DIM
    group = q_heads // kv_heads
    me = lax.axis_index("cp")
    chip = me // 2
    core = lax.rem(me, 2)
    sib = chip * 2 + (1 - core)
    par = (1 - chip) * 2 + core
    dia = (1 - chip) * 2 + (1 - core)
    last = 2 * CP_SIZE - 1

    w_copies = [pltpu.make_async_copy(src, dst, wsem.at[i]) for i, (src, dst) in enumerate(((wk_hbm, wk), (wv_hbm, wv), (wq_hbm, wq), (wo_hbm, wo)))]

    def x_copy(b):
        return pltpu.make_async_copy(x_hbm.at[b], xb.at[b], xsem.at[b])

    def y_copy(b):
        return pltpu.make_async_copy(xb.at[b], y_hbm.at[b], ysem.at[b])

    w_copies[0].start()
    x_copy(0).start()
    w_copies[1].start()
    for b in range(1, 3):
        x_copy(b).start()
    w_copies[2].start()
    for b in range(3, rows):
        x_copy(b).start()
    w_copies[3].start()

    barrier = pltpu.get_barrier_semaphore()
    for other in (sib, par):
        pl.semaphore_signal(barrier, inc=1, device_id={"cp": other}, device_id_type=MESH)
    pl.semaphore_wait(barrier, 2)

    def block(b, idx):
        return kv.at[b, pl.ds(pl.multiple_of(idx * BLK, BLK), BLK), :]

    def remote(b, idx, half, send, recv, dev):
        return pltpu.make_async_remote_copy(src_ref=block(b, idx), dst_ref=block(b, idx), send_sem=send.at[half, b], recv_sem=recv.at[half, b], device_id={"cp": dev}, device_id_type=MESH)

    def send_row(b):
        remote(b, me, 0, ici_s, ici_r, par).start()

        @pl.when(chip == 1)
        def _():
            remote(b, last - me, 1, ici_s, ici_r, par).start()

        remote(b, me, 0, sib_s, sib_r, sib).start()

        @pl.when(core == 1)
        def _():
            remote(b, last - me, 1, sib_s, sib_r, sib).start()

    def make_kv(b):
        angles = freq_ref[...] * pos_ref[pl.ds(b, 1), :].astype(jnp.float32)
        cosine, sine = jnp.cos(angles), jnp.sin(angles)
        cos_tab = jnp.concatenate([cosine, cosine], axis=0).T
        sin_tab = jnp.concatenate([-sine, sine], axis=0).T
        cos_b[b] = cos_tab
        sin_b[b] = sin_tab
        x_row = xb[b]
        k_row = jnp.dot(x_row, wk[...], preferred_element_type=jnp.float32).astype(jnp.bfloat16)
        v_row = jnp.dot(x_row, wv[...], preferred_element_type=jnp.float32).astype(jnp.bfloat16)
        for half, idx in ((0, me), (1, last - me)):
            lo = half * BLK
            dst = pl.ds(pl.multiple_of(idx * BLK, BLK), BLK)
            for h in range(kv_heads):
                cols = slice(h * HEAD_DIM, (h + 1) * HEAD_DIM)
                kv[b, dst, cols] = rope_head(k_row[lo:lo + BLK, cols], cos_tab[lo:lo + BLK], sin_tab[lo:lo + BLK])
            kv[b, dst, kv_cols:] = v_row[lo:lo + BLK]

    def make_q(b, slot):
        x_row = xb[b]
        cos_tab, sin_tab = cos_b[b], sin_b[b]
        for n in range(0, q_heads, 2):
            pair = jnp.dot(x_row, wq[:, n * HEAD_DIM:(n + 2) * HEAD_DIM], preferred_element_type=jnp.float32).astype(jnp.bfloat16)
            for i in range(2):
                qb[slot, n + i] = rope_head(pair[:, i * HEAD_DIM:(i + 1) * HEAD_DIM], cos_tab, sin_tab)

    def attend(b, slot, dev):
        tri = lax.broadcasted_iota(jnp.int32, (2 * BLK, BLK), 1) <= lax.rem(lax.broadcasted_iota(jnp.int32, (2 * BLK, BLK), 0), BLK)
        for g in range(kv_heads):
            for half, n_blk in ((1, last - dev + 1), (0, dev + 1)):
                n_key = n_blk * BLK
                toks_at = slice(half * BLK, (half + 1) * BLK)
                keys = kv[b, 0:n_key, g * HEAD_DIM:(g + 1) * HEAD_DIM]
                vals = kv[b, 0:n_key, kv_cols + g * HEAD_DIM:kv_cols + (g + 1) * HEAD_DIM]
                for h in range(g * group, (g + 1) * group, 2):
                    q_pair = qb[slot, h:h + 2, toks_at, :].reshape(2 * BLK, HEAD_DIM)
                    scores = nt_dot(q_pair, keys)
                    diag = jnp.where(tri, scores[:, n_key - BLK:], MASK_FILL)
                    scores = diag if n_blk == 1 else jnp.concatenate([scores[:, :n_key - BLK], diag], axis=1)
                    top = jnp.max(scores, axis=1, keepdims=True)
                    exp_w = jnp.exp2((scores - top) * EXP_SCALE)
                    inv = 1.0 / jnp.sum(exp_w, axis=1, keepdims=True)
                    out = (jnp.dot(exp_w.astype(jnp.bfloat16), vals, preferred_element_type=jnp.float32) * inv).astype(jnp.bfloat16)
                    for i in range(2):
                        ob[toks_at, (h + i) * HEAD_DIM:(h + i + 1) * HEAD_DIM] = out[i * BLK:(i + 1) * BLK]

    def project_out(b):
        o_row = ob[...]
        for n in range(0, width, 2 * HEAD_DIM):
            cols = slice(n, n + 2 * HEAD_DIM)
            y_part = jnp.dot(o_row, wo[:, cols], preferred_element_type=jnp.float32)
            xb[b, :, cols] = (xb[b, :, cols].astype(jnp.float32) + y_part).astype(jnp.bfloat16)
        y_copy(b).start()

    w_copies[0].wait()
    w_copies[1].wait()

    def kv_step(b, _):
        x_copy(b).wait()
        make_kv(b)

        @pl.when(b > 0)
        def _():
            send_row(b - 1)

        return _

    lax.fori_loop(0, rows, kv_step, None)
    send_row(rows - 1)
    w_copies[2].wait()
    make_q(0, 0)
    w_copies[3].wait()

    def row_step(b, _):
        slot = lax.rem(b, 2)
        remote(b, par, 0, ici_s, ici_r, par).wait_recv()
        remote(b, par, 0, fwd_s, fwd_r, sib).start()

        @pl.when(chip == 0)
        def _():
            remote(b, last - par, 1, ici_s, ici_r, par).wait_recv()
            remote(b, last - par, 1, fwd_s, fwd_r, sib).start()

        @pl.when(b < rows - 1)
        def _():
            make_q(b + 1, 1 - slot)

        remote(b, sib, 0, sib_s, sib_r, sib).wait_recv()

        @pl.when(core == 0)
        def _():
            remote(b, last - sib, 1, sib_s, sib_r, sib).wait_recv()

        remote(b, dia, 0, fwd_s, fwd_r, sib).wait_recv()

        @pl.when(chip == 0)
        def _():
            remote(b, last - dia, 1, fwd_s, fwd_r, sib).wait_recv()

        for dev in range(CP_SIZE):
            @pl.when(me == dev)
            def _():
                attend(b, slot, dev)

        project_out(b)
        return _

    lax.fori_loop(0, rows, row_step, None)

    def drain(b, _):
        y_copy(b).wait()
        remote(b, me, 0, ici_s, ici_r, par).wait_send()
        remote(b, me, 0, sib_s, sib_r, sib).wait_send()
        remote(b, par, 0, fwd_s, fwd_r, sib).wait_send()

        @pl.when(chip == 1)
        def _():
            remote(b, last - me, 1, ici_s, ici_r, par).wait_send()

        @pl.when(core == 1)
        def _():
            remote(b, last - me, 1, sib_s, sib_r, sib).wait_send()

        @pl.when(chip == 0)
        def _():
            remote(b, last - par, 1, fwd_s, fwd_r, sib).wait_send()

        return _

    lax.fori_loop(0, rows, drain, None)


def solution(mesh):
    row_spec = P('data', 'cp', None)
    pos_spec = P('data', 'cp')
    rep_spec = P(None, None)

    def local_block(x_loc, pos_loc, w_query, w_key, w_value, w_out):
        rows, toks, width = x_loc.shape
        q_cols, kv_cols = w_query.shape[1], w_key.shape[1]
        inv_freq = 1.0 / (ROPE_BASE ** (jnp.arange(0, HEAD_DIM, 2, dtype=jnp.float32) / HEAD_DIM))
        freq = jnp.broadcast_to(inv_freq[:, None], (HALF_DIM, toks))
        any_spec = pl.BlockSpec(memory_space=pl.ANY)
        vmem_spec = pl.BlockSpec(memory_space=pltpu.VMEM)
        bf16, f32 = jnp.bfloat16, jnp.float32
        pair_sem = pltpu.SemaphoreType.DMA((2, rows))
        row_sem = pltpu.SemaphoreType.DMA((rows,))
        return pl.pallas_call(
            kernel,
            out_shape=jax.ShapeDtypeStruct(x_loc.shape, bf16),
            in_specs=[any_spec, vmem_spec, vmem_spec] + [any_spec] * 4,
            out_specs=any_spec,
            scratch_shapes=[
                pltpu.VMEM((rows, toks, width), bf16),
                pltpu.VMEM((width, q_cols), bf16),
                pltpu.VMEM((width, kv_cols), bf16),
                pltpu.VMEM((width, kv_cols), bf16),
                pltpu.VMEM((q_cols, width), bf16),
                pltpu.VMEM((rows, CP_SIZE * toks, 2 * kv_cols), bf16),
                pltpu.VMEM((2, q_cols // HEAD_DIM, toks, HEAD_DIM), bf16),
                pltpu.VMEM((toks, q_cols), bf16),
                pltpu.VMEM((rows, toks, HEAD_DIM), f32),
                pltpu.VMEM((rows, toks, HEAD_DIM), f32),
                row_sem, pltpu.SemaphoreType.DMA((4,)), row_sem,
                pair_sem, pair_sem, pair_sem, pair_sem, pair_sem, pair_sem,
            ],
            compiler_params=pltpu.CompilerParams(collective_id=0, has_side_effects=True, vmem_limit_bytes=62 * 1024 * 1024),
        )(x_loc, pos_loc, freq, w_query, w_key, w_value, w_out)

    return jax.shard_map(local_block, mesh=mesh, in_specs=(row_spec, pos_spec, rep_spec, rep_spec, rep_spec, rep_spec), out_specs=row_spec, check_vma=False)
```

time: 649 us -> 150 us (0.23)
  the two profiles are of different devices: /device:TPU:0 before, /device:TPU:3 now
where the time goes in v1:
time: 150 us
  Pallas kernels  139 us (93%)
  local copies, waits for them, and re-layouts  11.2 us (7%)
    pallas_call x1, Pallas kernels, local_block(): pl.pallas_call(kernel, out_shape=jax.ShapeDtypeStruct(x_loc.shape, bf16),...  139 us
    unnamed x1, local copies, waits for them, and re-layouts  10.5 us

profile of v1, /device:TPU:3, one launch (start us, length us, event | category | flops | bytes accessed | tf_op | source)
XLA Modules:
  0.0 149.8 jit_solution(10024105841903607944)
XLA Ops:
  0.0 0.7 broadcast_in_dim.2.freq_ref
  0.7 138.6 %shard_map.64 = bf16[16,256,1536]{2,1,0:T(8,128)(2,1)} custom-call(bf16[16,256,1536]{2,1,0:T(8,128)(2,1)} %x_hbm.1, s32[16,256]{1,0:T(8,128)} %pos_ref.1, f32[64,256]{1,0:T(8,128)} %broadcast_in_dim.2.freq_ref, bf16[1536,1536]{1,0:T(8,128)(2,1)} %wq_hbm.1, bf16[1536,256]{1,0:T(8,128)(2,1)} %wk_hbm.1, bf16[1536,256]{1,0:T(8,128)(2,1)} %wv_hbm.1, ...), custom_call_target="tpu_custom_call" | custom-call | tf_op jit(solution)/shard_map/pallas_call | solution.py:235
  139.3 10.5 %copy.8 = bf16[16,256,1536]{2,1,0:T(8,128)(2,1)} copy(bf16[16,256,1536]{2,1,0:T(8,128)(2,1)} %shard_map.64) | data formatting | bytes 25165824
  (1 shorter events, 0.0 us)

commit v2 on v1

v2 whole, which is shorter than its diff:
```python
import functools
import math

import jax
import jax.numpy as jnp
import numpy as np
from jax import lax
from jax.experimental import pallas as pl
from jax.experimental.pallas import tpu as pltpu
from jax.sharding import PartitionSpec as P

HEAD_DIM = 128
HALF_DIM = HEAD_DIM // 2
ROPE_BASE = 500000
MASK_FILL = -1e30
EXP_SCALE = math.log2(math.e) * HEAD_DIM ** -0.5
CP_SIZE = 4
BLK = 128
MESH = pl.DeviceIdType.MESH
TURN = 2.0 ** 32
SIN_COEF = [(-1) ** k * (2 * math.pi) ** (2 * k + 1) / math.factorial(2 * k + 1) for k in range(7)]


def turn_tables(toks):
    turns = ROPE_BASE ** (-np.arange(0, HEAD_DIM, 2, dtype=np.float64) / HEAD_DIM) / (2 * math.pi)
    high = np.floor(turns * TURN)
    low = turns - high / TURN
    sub = 8
    lane_row = lax.broadcasted_iota(jnp.int32, (sub, toks), 0)
    parts = ([], [])
    for a in range(0, HALF_DIM, sub):
        for part, values, kind, num in zip(parts, (high, low), (jnp.int32, jnp.float32), (int, float)):
            tile = jnp.full((sub, toks), num(values[a]), kind)
            for c in range(1, sub):
                tile = jnp.where(lane_row == c, jnp.full((sub, toks), num(values[a + c]), kind), tile)
            part.append(tile)
    return [jnp.concatenate(part, axis=0) for part in parts]


def sin_turns(part):
    square = part * part
    total = jnp.full_like(part, SIN_COEF[-1])
    for coef in SIN_COEF[-2::-1]:
        total = total * square + coef
    return total * part


def nt_dot(lhs, rhs):
    return lax.dot_general(lhs, rhs, (((1,), (1,)), ((), ())), preferred_element_type=jnp.float32)


def rope_head(head, cos_tab, sin_tab):
    wide = head.astype(jnp.float32)
    return (wide * cos_tab + pltpu.roll(wide, HALF_DIM, 1) * sin_tab).astype(jnp.bfloat16)


def kernel(x_hbm, pos_ref, wq_hbm, wk_hbm, wv_hbm, wo_hbm, xb,
           wq, wk, wv, wo, kv, qb, ob, sb, high_b, low_b, cos_b, sin_b,
           xsem, wsem, ici_s, ici_r, sib_s, sib_r, fwd_s, fwd_r):
    rows, toks, width = xb.shape
    kv_cols = wk.shape[1]
    kv_heads = kv_cols // HEAD_DIM
    q_heads = wq.shape[1] // HEAD_DIM
    group = q_heads // kv_heads
    me = lax.axis_index("cp")
    chip = me // 2
    core = lax.rem(me, 2)
    sib = chip * 2 + (1 - core)
    par = (1 - chip) * 2 + core
    dia = (1 - chip) * 2 + (1 - core)
    last = 2 * CP_SIZE - 1

    w_copies = [pltpu.make_async_copy(src, dst, wsem.at[i]) for i, (src, dst) in enumerate(((wk_hbm, wk), (wv_hbm, wv), (wq_hbm, wq), (wo_hbm, wo)))]

    def x_copy(b):
        return pltpu.make_async_copy(x_hbm.at[b], xb.at[b], xsem.at[b])

    def w_piece(src, dst, i, at):
        depth = src.shape[0] // (rows // 2)
        part = pl.ds(pl.multiple_of(at * depth, depth), depth)
        return pltpu.make_async_copy(src.at[part], dst.at[part], wsem.at[i])

    w_copies[0].start()
    x_copy(0).start()
    w_copies[1].start()
    x_copy(1).start()
    high_b[...], low_b[...] = turn_tables(toks)
    barrier = pltpu.get_barrier_semaphore()
    for other in (sib, par):
        pl.semaphore_signal(barrier, inc=1, device_id={"cp": other}, device_id_type=MESH)
    pl.semaphore_wait(barrier, 2)

    def block(b, idx):
        return kv.at[b, idx]

    def remote(b, idx, half, send, recv, dev):
        return pltpu.make_async_remote_copy(src_ref=block(b, idx), dst_ref=block(b, idx), send_sem=send.at[half, b], recv_sem=recv.at[half, b], device_id={"cp": dev}, device_id_type=MESH)

    def send_row(b):
        remote(b, me, 0, ici_s, ici_r, par).start()

        @pl.when(chip == 1)
        def _():
            remote(b, last - me, 1, ici_s, ici_r, par).start()

        remote(b, me, 0, sib_s, sib_r, sib).start()

        @pl.when(core == 1)
        def _():
            remote(b, last - me, 1, sib_s, sib_r, sib).start()

    def make_kv(b):
        pos = pos_ref[pl.ds(b, 1), :]
        turns = (pos * high_b[...]).astype(jnp.float32) * (1.0 / TURN) + pos.astype(jnp.float32) * low_b[...]
        turns = turns - jnp.round(turns)
        size = jnp.abs(turns)
        cosine = sin_turns(0.25 - size)
        sine = sin_turns(jnp.minimum(size, 0.5 - size))
        sine = jnp.where(turns < 0, -sine, sine)
        cos_tab = jnp.concatenate([cosine, cosine], axis=0).T
        sin_tab = jnp.concatenate([-sine, sine], axis=0).T
        cos_b[b] = cos_tab
        sin_b[b] = sin_tab
        x_row = xb[b]
        k_row = jnp.dot(x_row, wk[...], preferred_element_type=jnp.float32).astype(jnp.bfloat16)
        v_row = jnp.dot(x_row, wv[...], preferred_element_type=jnp.float32)
        for half, idx in ((0, me), (1, last - me)):
            lo = half * BLK
            for h in range(kv_heads):
                cols = slice(h * HEAD_DIM, (h + 1) * HEAD_DIM)
                kv[b, idx, cols, :] = rope_head(k_row[lo:lo + BLK, cols], cos_tab[lo:lo + BLK], sin_tab[lo:lo + BLK])
                kv[b, idx, kv_cols + h * HEAD_DIM:kv_cols + (h + 1) * HEAD_DIM, :] = v_row[lo:lo + BLK, cols].T.astype(jnp.bfloat16)

    def make_q(b, slot):
        x_row = xb[b]
        cos_tab, sin_tab = cos_b[b], sin_b[b]
        for n in range(0, q_heads, 2):
            pair = jnp.dot(x_row, wq[:, n * HEAD_DIM:(n + 2) * HEAD_DIM], preferred_element_type=jnp.float32).astype(jnp.bfloat16)
            for i in range(2):
                qb[slot, n + i] = rope_head(pair[:, i * HEAD_DIM:(i + 1) * HEAD_DIM], cos_tab, sin_tab)

    def attend(b, slot, dev, fill):
        wide = (BLK, 2 * BLK)
        tri = lax.broadcasted_iota(jnp.int32, wide, 0) <= lax.rem(lax.broadcasted_iota(jnp.int32, wide, 1), BLK)
        units = [(half, g, h) for half in (1, 0) for g in range(kv_heads) for h in range(g * group, (g + 1) * group, 2)]

        def spans(half):
            n_blk = last - dev + 1 if half else dev + 1
            return n_blk, n_blk * BLK, slice(half * BLK, (half + 1) * BLK)

        def score(k):
            half, g, h = units[k]
            n_blk, n_key, toks_at = spans(half)
            keys = kv[b, 0:n_blk, g * HEAD_DIM:(g + 1) * HEAD_DIM, :].reshape(n_key, HEAD_DIM)
            scores = nt_dot(keys, qb[slot, h:h + 2, toks_at, :].reshape(2 * BLK, HEAD_DIM))
            diag = jnp.where(tri, scores[n_key - BLK:], MASK_FILL)
            sb[k % 2, n_key - BLK:n_key, :] = diag
            top = jnp.max(diag, axis=0, keepdims=True)
            if n_blk > 1:
                sb[k % 2, 0:n_key - BLK, :] = scores[:n_key - BLK]
                top = jnp.maximum(top, jnp.max(scores[:n_key - BLK], axis=0, keepdims=True))
            return top

        def weigh(k, top):
            half, g, h = units[k]
            n_blk, n_key, toks_at = spans(half)
            exp_w = jnp.exp2((sb[k % 2, 0:n_key, :] - top) * EXP_SCALE)
            inv = 1.0 / jnp.sum(exp_w, axis=0, keepdims=True)
            rows_at = slice(kv_cols + g * HEAD_DIM, kv_cols + (g + 1) * HEAD_DIM)
            vals = jnp.concatenate([kv[b, i, rows_at, :] for i in range(n_blk)], axis=1)
            out = (jnp.dot(vals, exp_w.astype(jnp.bfloat16), preferred_element_type=jnp.float32) * inv).T.astype(jnp.bfloat16)
            for i in range(2):
                ob[slot, toks_at, (h + i) * HEAD_DIM:(h + i + 1) * HEAD_DIM] = out[i * BLK:(i + 1) * BLK]

        top = score(0)
        for k in range(len(units)):
            ahead = score(k + 1) if k + 1 < len(units) else None
            weigh(k, top)
            top = ahead
            fill(k, len(units))

    def out_tile(b, slot, n, keep):
        cols = slice(n * 2 * HEAD_DIM, (n + 1) * 2 * HEAD_DIM)
        y_part = jnp.dot(ob[slot], wo[:, cols], preferred_element_type=jnp.float32)
        if keep is not None:
            y_part = jnp.where(keep, y_part, 0.0)
        xb[b, :, cols] = (xb[b, :, cols].astype(jnp.float32) + y_part).astype(jnp.bfloat16)

    out_tiles = width // (2 * HEAD_DIM)

    w_copies[0].wait()
    w_copies[1].wait()

    def kv_step(b, _):
        @pl.when(b < rows - 2)
        def _():
            x_copy(b + 2).start()

        @pl.when(b < rows // 2)
        def _():
            w_piece(wq_hbm, wq, 2, b).start()

        @pl.when(b >= rows // 2)
        def _():
            w_piece(wo_hbm, wo, 3, b - rows // 2).start()

        x_copy(b).wait()
        make_kv(b)

        @pl.when(b > 0)
        def _():
            send_row(b - 1)

        return _

    lax.fori_loop(0, rows, kv_step, None)
    send_row(rows - 1)
    w_copies[2].wait()
    make_q(0, 0)
    w_copies[3].wait()

    def row_step(b, _):
        slot = lax.rem(b, 2)
        remote(b, par, 0, ici_s, ici_r, par).wait_recv()
        remote(b, par, 0, fwd_s, fwd_r, sib).start()

        @pl.when(chip == 0)
        def _():
            remote(b, last - par, 1, ici_s, ici_r, par).wait_recv()
            remote(b, last - par, 1, fwd_s, fwd_r, sib).start()

        @pl.when(b < rows - 1)
        def _():
            make_q(b + 1, 1 - slot)

        remote(b, sib, 0, sib_s, sib_r, sib).wait_recv()

        @pl.when(core == 0)
        def _():
            remote(b, last - sib, 1, sib_s, sib_r, sib).wait_recv()

        remote(b, dia, 0, fwd_s, fwd_r, sib).wait_recv()

        @pl.when(chip == 0)
        def _():
            remote(b, last - dia, 1, fwd_s, fwd_r, sib).wait_recv()

        def fill(k, count):
            if (k + 1) * out_tiles // count > k * out_tiles // count:
                out_tile(jnp.maximum(b - 1, 0), 1 - slot, k * out_tiles // count, b > 0)

        for dev in range(CP_SIZE):
            @pl.when(me == dev)
            def _():
                attend(b, slot, dev, fill)

        return _

    lax.fori_loop(0, rows, row_step, None)
    for n in range(out_tiles):
        out_tile(rows - 1, (rows - 1) % 2, n, None)

    def drain(b, _):
        remote(b, me, 0, ici_s, ici_r, par).wait_send()
        remote(b, me, 0, sib_s, sib_r, sib).wait_send()
        remote(b, par, 0, fwd_s, fwd_r, sib).wait_send()

        @pl.when(chip == 1)
        def _():
            remote(b, last - me, 1, ici_s, ici_r, par).wait_send()

        @pl.when(core == 1)
        def _():
            remote(b, last - me, 1, sib_s, sib_r, sib).wait_send()

        @pl.when(chip == 0)
        def _():
            remote(b, last - par, 1, fwd_s, fwd_r, sib).wait_send()

        return _

    lax.fori_loop(0, rows, drain, None)


def put_kernel(y_vmem, y_hbm, sem):
    rows = y_vmem.shape[0]
    copies = [pltpu.make_async_copy(y_vmem.at[b], y_hbm.at[b], sem.at[b]) for b in range(rows)]
    for copy in copies:
        copy.start()
    for copy in copies:
        copy.wait()


def put_out(y_vmem):
    return pl.pallas_call(
        put_kernel,
        out_shape=jax.ShapeDtypeStruct(y_vmem.shape, y_vmem.dtype),
        in_specs=[pl.BlockSpec(memory_space=pltpu.VMEM)],
        out_specs=pl.BlockSpec(memory_space=pl.ANY),
        scratch_shapes=[pltpu.SemaphoreType.DMA((y_vmem.shape[0],))],
        compiler_params=pltpu.CompilerParams(vmem_limit_bytes=14 * 1024 * 1024),
    )(y_vmem)


def solution(mesh):
    row_spec = P('data', 'cp', None)
    pos_spec = P('data', 'cp')
    rep_spec = P(None, None)

    def local_block(x_loc, pos_loc, w_query, w_key, w_value, w_out):
        rows, toks, width = x_loc.shape
        q_cols, kv_cols = w_query.shape[1], w_key.shape[1]
        any_spec = pl.BlockSpec(memory_space=pl.ANY)
        vmem_spec = pl.BlockSpec(memory_space=pltpu.VMEM)
        bf16, f32 = jnp.bfloat16, jnp.float32
        pair_sem = pltpu.SemaphoreType.DMA((2, rows))
        row_sem = pltpu.SemaphoreType.DMA((rows,))
        y_vmem = pl.pallas_call(
            kernel,
            out_shape=pltpu.VMEM(x_loc.shape, bf16),
            in_specs=[any_spec, vmem_spec] + [any_spec] * 4,
            out_specs=vmem_spec,
            scratch_shapes=[
                pltpu.VMEM((width, q_cols), bf16),
                pltpu.VMEM((width, kv_cols), bf16),
                pltpu.VMEM((width, kv_cols), bf16),
                pltpu.VMEM((q_cols, width), bf16),
                pltpu.VMEM((rows, 2 * CP_SIZE, 2 * kv_cols, BLK), bf16),
                pltpu.VMEM((2, q_cols // HEAD_DIM, toks, HEAD_DIM), bf16),
                pltpu.VMEM((2, toks, q_cols), bf16),
                pltpu.VMEM((2, CP_SIZE * toks, 2 * BLK), f32),
                pltpu.VMEM((HALF_DIM, toks), jnp.int32),
                pltpu.VMEM((HALF_DIM, toks), f32),
                pltpu.VMEM((rows, toks, HEAD_DIM), f32),
                pltpu.VMEM((rows, toks, HEAD_DIM), f32),
                row_sem, pltpu.SemaphoreType.DMA((4,)),
                pair_sem, pair_sem, pair_sem, pair_sem, pair_sem, pair_sem,
            ],
            compiler_params=pltpu.CompilerParams(collective_id=0, has_side_effects=True, vmem_limit_bytes=48 * 1024 * 1024),
        )(x_loc, pos_loc, w_query, w_key, w_value, w_out)
        return put_out(y_vmem)

    return jax.shard_map(local_block, mesh=mesh, in_specs=(row_spec, pos_spec, rep_spec, rep_spec, rep_spec, rep_spec), out_specs=row_spec, check_vma=False)
```

time: 150 us -> 114 us (0.76)
  the two profiles are of different devices: /device:TPU:3 before, /device:TPU:0 now
where the time goes in v2:
time: 114 us; the launch traced here: 113 us
  Pallas kernels  113 us (99%)
    pallas_call x1, Pallas kernels, local_block(): pl.pallas_call(kernel, out_shape=pltpu.VMEM(x_loc.shape, bf16), in_specs=...  109 us
    pallas_call x1, Pallas kernels, put_out(): pl.pallas_call(put_kernel, out_shape=jax.ShapeDtypeStruct(y_vmem.shape, y...  4.7 us

profile of v2, /device:TPU:0, one launch (start us, length us, event | category | flops | bytes accessed | tf_op | source)
XLA Modules:
  0.0 113.3 jit_solution(10313952027180303059)
XLA Ops:
  0.0 108.6 %shard_map.64.y_vmem = bf16[16,256,1536]{2,1,0:T(8,128)(2,1)S(1)} custom-call(bf16[16,256,1536]{2,1,0:T(8,128)(2,1)} %x_hbm.1, s32[16,256]{1,0:T(8,128)} %pos_ref.1, bf16[1536,1536]{1,0:T(8,128)(2,1)} %wq_hbm.1, bf16[1536,256]{1,0:T(8,128)(2,1)} %wk_hbm.1, bf16[1536,256]{1,0:T(8,128)(2,1)} %wv_hbm.1, bf16[1536,1536]{1,0:T(8,128)(2,1)} %wo_hbm.1), custom_call_target="tpu_custom_call" | custom-call | tf_op jit(solution)/shard_map/pallas_call | solution.py:318
  108.6 4.7 %shard_map.65 = bf16[16,256,1536]{2,1,0:T(8,128)(2,1)} custom-call(bf16[16,256,1536]{2,1,0:T(8,128)(2,1)S(1)} %shard_map.64.y_vmem), custom_call_target="tpu_custom_call" | custom-call | tf_op jit(solution)/shard_map/pallas_call | solution.py:295

commit v3 on v2

v3 whole, which is shorter than its diff:
```python
import math

import jax
import jax.numpy as jnp
import numpy as np
from jax import lax
from jax.experimental import pallas as pl
from jax.experimental.pallas import tpu as pltpu
from jax.sharding import PartitionSpec as P

HEAD_DIM = 128
HALF_DIM = HEAD_DIM // 2
ROPE_BASE = 500000
MASK_FILL = -1e30
EXP_SCALE = math.log2(math.e) * HEAD_DIM ** -0.5
CP_SIZE = 4
LAST = 2 * CP_SIZE - 1
BLK = 128
LEAD = 2
MESH = pl.DeviceIdType.MESH
TURN = 2.0 ** 32
SIN_COEF = [(-1) ** k * (2 * math.pi) ** (2 * k + 1) / math.factorial(2 * k + 1) for k in range(7)]


def turn_tables(toks):
    turns = ROPE_BASE ** (-np.arange(0, HEAD_DIM, 2, dtype=np.float64) / HEAD_DIM) / (2 * math.pi)
    high = np.floor(turns * TURN)
    low = turns - high / TURN
    sub = 8
    lane_row = lax.broadcasted_iota(jnp.int32, (sub, toks), 0)
    parts = ([], [])
    for a in range(0, HALF_DIM, sub):
        for part, values, kind, num in zip(parts, (high, low), (jnp.int32, jnp.float32), (int, float)):
            tile = jnp.full((sub, toks), num(values[a]), kind)
            for c in range(1, sub):
                tile = jnp.where(lane_row == c, jnp.full((sub, toks), num(values[a + c]), kind), tile)
            part.append(tile)
    return [jnp.concatenate(part, axis=0) for part in parts]


def sin_turns(part):
    square = part * part
    total = jnp.full_like(part, SIN_COEF[-1])
    for coef in SIN_COEF[-2::-1]:
        total = total * square + coef
    return total * part


def nt_dot(lhs, rhs):
    return lax.dot_general(lhs, rhs, (((1,), (1,)), ((), ())), preferred_element_type=jnp.float32)


def rope_head(head, cos_tab, sin_tab):
    wide = head.astype(jnp.float32)
    return (wide * cos_tab + pltpu.roll(wide, HALF_DIM, 1) * sin_tab).astype(jnp.bfloat16)


def attend(kv_row, row_of, q_row, o_row, sb, group, dev, groups, fill):
    wide = (BLK, 2 * BLK)
    tri = lax.broadcasted_iota(jnp.int32, wide, 0) <= lax.rem(lax.broadcasted_iota(jnp.int32, wide, 1), BLK)
    units = [(half, g, h) for half in (1, 0) for g in groups for h in range(g * group, (g + 1) * group, 2)]

    def spans(half):
        n_blk = LAST - dev + 1 if half else dev + 1
        return n_blk, n_blk * BLK, slice(half * BLK, (half + 1) * BLK)

    starts, at = [], 0
    for half, _, _ in units:
        need = spans(half)[1]
        at = 0 if at + need > sb.shape[0] else at
        starts.append(at)
        at += need

    def score(k):
        half, g, h = units[k]
        n_blk, n_key, toks_at = spans(half)
        base = starts[k]
        keys = kv_row[0:n_blk, row_of(g):row_of(g) + BLK, :].reshape(n_key, HEAD_DIM)
        scores = nt_dot(keys, q_row[h:h + 2, toks_at, :].reshape(2 * BLK, HEAD_DIM))
        diag = jnp.where(tri, scores[n_key - BLK:], MASK_FILL)
        sb[base + n_key - BLK:base + n_key, :] = diag
        top = jnp.max(diag, axis=0, keepdims=True)
        if n_blk > 1:
            sb[base:base + n_key - BLK, :] = scores[:n_key - BLK]
            top = jnp.maximum(top, jnp.max(scores[:n_key - BLK], axis=0, keepdims=True))
        return top

    def weigh(k, top):
        half, g, h = units[k]
        n_blk, n_key, toks_at = spans(half)
        exp_w = jnp.exp2((sb[starts[k]:starts[k] + n_key, :] - top) * EXP_SCALE)
        inv = 1.0 / jnp.sum(exp_w, axis=0, keepdims=True)
        lo = row_of(g) + BLK
        vals = jnp.concatenate([kv_row[i, lo:lo + HEAD_DIM, :] for i in range(n_blk)], axis=1)
        out = (jnp.dot(vals, exp_w.astype(jnp.bfloat16), preferred_element_type=jnp.float32) * inv).T.astype(jnp.bfloat16)
        for i in range(2):
            o_row[toks_at, (h + i) * HEAD_DIM:(h + i + 1) * HEAD_DIM] = out[i * BLK:(i + 1) * BLK]

    count = len(units)
    tops = [score(k) for k in range(LEAD)]
    for k in range(count):
        if k + LEAD < count:
            tops.append(score(k + LEAD))
        weigh(k, tops[k])
        fill(k, count)


def main_kernel(x_hbm, pos_ref, wq_hbm, wk_hbm, wv_hbm, wo_hbm, xb, wo, kv_end, qb, ob,
                wq, wk, wv, kv, sb, high_b, low_b, cos_b, sin_b,
                xsem, wsem, ici_s, ici_r, sib_s, sib_r, fwd_s, fwd_r):
    rows, toks, width = xb.shape
    kv_cols = wk.shape[1]
    kv_heads = kv_cols // HEAD_DIM
    q_heads = wq.shape[1] // HEAD_DIM
    group = q_heads // kv_heads
    end = rows - 1
    me = lax.axis_index("cp")
    chip = me // 2
    core = lax.rem(me, 2)
    sib = chip * 2 + (1 - core)
    par = (1 - chip) * 2 + core
    dia = (1 - chip) * 2 + (1 - core)

    w_copies = [pltpu.make_async_copy(src, dst, wsem.at[i]) for i, (src, dst) in enumerate(((wk_hbm, wk), (wv_hbm, wv), (wq_hbm, wq), (wo_hbm, wo)))]

    def x_copy(b):
        return pltpu.make_async_copy(x_hbm.at[b], xb.at[b], xsem.at[b])

    def w_piece(src, dst, i, at, count):
        depth = src.shape[0] // count
        part = pl.ds(pl.multiple_of(at * depth, depth), depth)
        return pltpu.make_async_copy(src.at[part], dst.at[part], wsem.at[i])

    w_copies[0].start()
    x_copy(0).start()
    w_copies[1].start()
    high_b[...], low_b[...] = turn_tables(toks)

    barrier = pltpu.get_barrier_semaphore()
    for other in (sib, par):
        pl.semaphore_signal(barrier, inc=1, device_id={"cp": other}, device_id_type=MESH)
    pl.semaphore_wait(barrier, 2)

    def row_at(g):
        return g * (BLK + HEAD_DIM)

    def remote(b, idx, half, send, recv, dev, head=None):
        ref = kv.at[b, idx] if head is None else kv.at[b, idx, row_at(head):row_at(head + 1)]
        sem = b if head is None else b + head
        return pltpu.make_async_remote_copy(src_ref=ref, dst_ref=ref, send_sem=send.at[half, sem], recv_sem=recv.at[half, sem], device_id={"cp": dev}, device_id_type=MESH)

    def send_link(b, head=None):
        remote(b, me, 0, ici_s, ici_r, par, head).start()

        @pl.when(chip == 1)
        def _():
            remote(b, LAST - me, 1, ici_s, ici_r, par, head).start()

    def send_sib(b):
        remote(b, me, 0, sib_s, sib_r, sib).start()

        @pl.when(core == 1)
        def _():
            remote(b, LAST - me, 1, sib_s, sib_r, sib).start()

    def send_row(b):
        send_link(b)
        send_sib(b)

    def relay(b, head=None):
        remote(b, par, 0, ici_s, ici_r, par, head).wait_recv()
        remote(b, par, 0, fwd_s, fwd_r, sib, head).start()

        @pl.when(chip == 0)
        def _():
            remote(b, LAST - par, 1, ici_s, ici_r, par, head).wait_recv()
            remote(b, LAST - par, 1, fwd_s, fwd_r, sib, head).start()

    def wait_sib(b):
        remote(b, sib, 0, sib_s, sib_r, sib).wait_recv()

        @pl.when(core == 0)
        def _():
            remote(b, LAST - sib, 1, sib_s, sib_r, sib).wait_recv()

    def wait_relay(b, head=None):
        remote(b, dia, 0, fwd_s, fwd_r, sib, head).wait_recv()

        @pl.when(chip == 0)
        def _():
            remote(b, LAST - dia, 1, fwd_s, fwd_r, sib, head).wait_recv()

    def make_kv(b):
        pos = pos_ref[pl.ds(b, 1), :]
        turns = (pos * high_b[...]).astype(jnp.float32) * (1.0 / TURN) + pos.astype(jnp.float32) * low_b[...]
        turns = turns - jnp.round(turns)
        size = jnp.abs(turns)
        cosine = sin_turns(0.25 - size)
        sine = sin_turns(jnp.minimum(size, 0.5 - size))
        sine = jnp.where(turns < 0, -sine, sine)
        cos_tab = jnp.concatenate([cosine, cosine], axis=0).T
        sin_tab = jnp.concatenate([-sine, sine], axis=0).T
        cos_b[b] = cos_tab
        sin_b[b] = sin_tab
        x_row = xb[b]
        k_row = jnp.dot(x_row, wk[...], preferred_element_type=jnp.float32).astype(jnp.bfloat16)
        v_row = jnp.dot(x_row, wv[...], preferred_element_type=jnp.float32)
        for half, idx in ((0, me), (1, LAST - me)):
            lo = half * BLK
            for g in range(kv_heads):
                cols = slice(g * HEAD_DIM, (g + 1) * HEAD_DIM)
                at = row_at(g)
                kv[b, idx, at:at + BLK, :] = rope_head(k_row[lo:lo + BLK, cols], cos_tab[lo:lo + BLK], sin_tab[lo:lo + BLK])
                kv[b, idx, at + BLK:at + BLK + HEAD_DIM, :] = v_row[lo:lo + BLK, cols].T.astype(jnp.bfloat16)

    def make_q(b, slot):
        x_row = xb[b]
        cos_tab, sin_tab = cos_b[b], sin_b[b]
        for n in range(0, q_heads, 2):
            pair = jnp.dot(x_row, wq[:, n * HEAD_DIM:(n + 2) * HEAD_DIM], preferred_element_type=jnp.float32).astype(jnp.bfloat16)
            for i in range(2):
                qb[slot, n + i] = rope_head(pair[:, i * HEAD_DIM:(i + 1) * HEAD_DIM], cos_tab, sin_tab)

    out_tiles = width // (2 * HEAD_DIM)

    def out_tile(b, slot, n, keep):
        cols = slice(n * 2 * HEAD_DIM, (n + 1) * 2 * HEAD_DIM)
        y_part = jnp.dot(ob[slot], wo[:, cols], preferred_element_type=jnp.float32)
        if keep is not None:
            y_part = jnp.where(keep, y_part, 0.0)
        xb[b, :, cols] = (xb[b, :, cols].astype(jnp.float32) + y_part).astype(jnp.bfloat16)

    for b in range(1, 5):
        x_copy(b).start()
    w_copies[0].wait()
    x_copy(0).wait()
    w_copies[1].wait()
    make_kv(0)

    def kv_step(i, _):
        at = 2 * i + 1
        x_copy(at).wait()
        x_copy(at + 1).wait()

        @pl.when(i > 0)
        def _():
            send_row(at - 2)

        send_row(at - 1)
        for b in (at + 4, at + 5):
            @pl.when(b < rows)
            def _():
                x_copy(b).start()

        @pl.when(i < 3)
        def _():
            w_piece(wq_hbm, wq, 2, i, 3).start()

        @pl.when(i >= 3)
        def _():
            w_piece(wo_hbm, wo, 3, i - 3, 4).start()

        make_kv(at)
        make_kv(at + 1)
        return _

    lax.fori_loop(0, (rows - 2) // 2, kv_step, None)
    send_row(end - 2)
    send_row(end - 1)
    x_copy(end).wait()
    w_copies[2].wait()
    make_kv(end)
    make_q(0, 0)
    send_link(end, 0)
    send_link(end, 1)
    send_sib(end)
    w_copies[3].wait()

    def row_step(b, _):
        slot = lax.rem(b, 2)
        relay(b)
        make_q(b + 1, 1 - slot)
        wait_sib(b)
        wait_relay(b)

        def fill(k, count):
            if (k + 1) * out_tiles // count > k * out_tiles // count:
                out_tile(jnp.maximum(b - 1, 0), 1 - slot, k * out_tiles // count, b > 0)

        for dev in range(CP_SIZE):
            @pl.when(me == dev)
            def _():
                attend(kv.at[b], row_at, qb.at[slot], ob.at[slot], sb, group, dev, range(kv_heads), fill)

        return _

    lax.fori_loop(0, end, row_step, None)
    slot = end % 2
    relay(end, 0)
    for n in range(out_tiles):
        out_tile(end - 1, 1 - slot, n, None)
    wait_sib(end)
    wait_relay(end, 0)
    for dev in range(CP_SIZE):
        @pl.when(me == dev)
        def _():
            attend(kv.at[end], row_at, qb.at[slot], ob.at[slot], sb, group, dev, range(kv_heads - 1), lambda k, count: None)

    relay(end, 1)
    wait_relay(end, 1)
    kv_end[...] = kv[end, :, row_at(kv_heads - 1):row_at(kv_heads), :]

    def drain(b, head):
        remote(b, me, 0, ici_s, ici_r, par, head).wait_send()
        remote(b, par, 0, fwd_s, fwd_r, sib, head).wait_send()

        @pl.when(chip == 1)
        def _():
            remote(b, LAST - me, 1, ici_s, ici_r, par, head).wait_send()

        @pl.when(chip == 0)
        def _():
            remote(b, LAST - par, 1, fwd_s, fwd_r, sib, head).wait_send()

    def drain_sib(b):
        remote(b, me, 0, sib_s, sib_r, sib).wait_send()

        @pl.when(core == 1)
        def _():
            remote(b, LAST - me, 1, sib_s, sib_r, sib).wait_send()

    def drain_row(b, _):
        drain(b, None)
        drain_sib(b)
        return _

    lax.fori_loop(0, end, drain_row, None)
    drain(end, 0)
    drain(end, 1)
    drain_sib(end)


def end_kernel(xb, wo, kv_end, qb, ob, y_hbm, sb, o_new, acc, y_row, sem):
    rows, toks, width = xb.shape
    q_heads = qb.shape[1]
    kv_heads = 2
    group = q_heads // kv_heads
    end = rows - 1
    slot = end % 2
    me = lax.axis_index("cp")
    copies = [pltpu.make_async_copy(xb.at[b], y_hbm.at[b], sem.at[b]) for b in range(end)]
    for copy in copies:
        copy.start()
    old = (kv_heads - 1) * group * HEAD_DIM
    tile = 2 * HEAD_DIM
    out_tiles = width // tile

    def fill(k, count):
        for n in range(k * out_tiles // count, (k + 1) * out_tiles // count):
            cols = slice(n * tile, (n + 1) * tile)
            acc[:, cols] = xb[end, :, cols].astype(jnp.float32) + jnp.dot(ob[slot, :, :old], wo[:old, cols], preferred_element_type=jnp.float32)

    for dev in range(CP_SIZE):
        @pl.when(me == dev)
        def _():
            attend(kv_end, lambda g: 0, qb.at[slot], o_new, sb, group, dev, (kv_heads - 1,), fill)

    last_copies = []
    for n in range(out_tiles):
        cols = slice(n * tile, (n + 1) * tile)
        y_row[:, cols] = (acc[:, cols] + jnp.dot(o_new[:, old:], wo[old:, cols], preferred_element_type=jnp.float32)).astype(jnp.bfloat16)
        if n % 2:
            span = slice((n - 1) * tile, (n + 1) * tile)
            last_copies.append(pltpu.make_async_copy(y_row.at[:, span], y_hbm.at[end, :, span], sem.at[end + n // 2]))
            last_copies[-1].start()
    for copy in copies + last_copies:
        copy.wait()


def solution(mesh):
    row_spec = P('data', 'cp', None)
    pos_spec = P('data', 'cp')
    rep_spec = P(None, None)

    def local_block(x_loc, pos_loc, w_query, w_key, w_value, w_out):
        rows, toks, width = x_loc.shape
        q_cols, kv_cols = w_query.shape[1], w_key.shape[1]
        q_heads = q_cols // HEAD_DIM
        any_spec = pl.BlockSpec(memory_space=pl.ANY)
        vmem_spec = pl.BlockSpec(memory_space=pltpu.VMEM)
        bf16, f32 = jnp.bfloat16, jnp.float32
        pair_sem = pltpu.SemaphoreType.DMA((2, rows + 1))
        row_sem = pltpu.SemaphoreType.DMA((rows,))
        kept = pl.pallas_call(
            main_kernel,
            out_shape=[
                pltpu.VMEM(x_loc.shape, bf16),
                pltpu.VMEM((q_cols, width), bf16),
                pltpu.VMEM((2 * CP_SIZE, BLK + HEAD_DIM, BLK), bf16),
                pltpu.VMEM((2, q_heads, toks, HEAD_DIM), bf16),
                pltpu.VMEM((2, toks, q_cols), bf16),
            ],
            in_specs=[any_spec, vmem_spec] + [any_spec] * 4,
            out_specs=[vmem_spec] * 5,
            scratch_shapes=[
                pltpu.VMEM((width, q_cols), bf16),
                pltpu.VMEM((width, kv_cols), bf16),
                pltpu.VMEM((width, kv_cols), bf16),
                pltpu.VMEM((rows, 2 * CP_SIZE, 2 * kv_cols, BLK), bf16),
                pltpu.VMEM((4 * CP_SIZE * toks, 2 * BLK), f32),
                pltpu.VMEM((HALF_DIM, toks), jnp.int32),
                pltpu.VMEM((HALF_DIM, toks), f32),
                pltpu.VMEM((rows, toks, HEAD_DIM), f32),
                pltpu.VMEM((rows, toks, HEAD_DIM), f32),
                row_sem, pltpu.SemaphoreType.DMA((4,)),
                pair_sem, pair_sem, pair_sem, pair_sem, pair_sem, pair_sem,
            ],
            compiler_params=pltpu.CompilerParams(collective_id=0, has_side_effects=True, vmem_limit_bytes=36 * 1024 * 1024),
        )(x_loc, pos_loc, w_query, w_key, w_value, w_out)
        return pl.pallas_call(
            end_kernel,
            out_shape=jax.ShapeDtypeStruct(x_loc.shape, bf16),
            in_specs=[vmem_spec] * 5,
            out_specs=any_spec,
            scratch_shapes=[
                pltpu.VMEM((4 * CP_SIZE * toks, 2 * BLK), f32),
                pltpu.VMEM((toks, q_cols), bf16),
                pltpu.VMEM((toks, width), f32),
                pltpu.VMEM((toks, width), bf16),
                pltpu.SemaphoreType.DMA((rows + 2,)),
            ],
            compiler_params=pltpu.CompilerParams(vmem_limit_bytes=16 * 1024 * 1024),
        )(*kept)

    return jax.shard_map(local_block, mesh=mesh, in_specs=(row_spec, pos_spec, rep_spec, rep_spec, rep_spec, rep_spec), out_specs=row_spec, check_vma=False)
```

time: 114 us -> 108 us (0.947)
  Pallas kernels: 113 us -> 108 us
    pallas_call x2, Pallas kernels: 113 us -> 108 us  [the longest x1 103 us: local_block(): pl.pallas_call(main_kernel, out_shape=[pltpu.VMEM(x_loc.shape, bf16), plt...]
where the time goes in v3:
time: 108 us
  Pallas kernels  108 us (100%)
    pallas_call x1, Pallas kernels, local_block(): pl.pallas_call(main_kernel, out_shape=[pltpu.VMEM(x_loc.shape, bf16), plt...  103 us
    pallas_call x1, Pallas kernels, local_block(): pl.pallas_call(end_kernel, out_shape=jax.ShapeDtypeStruct(x_loc.shape, bf...  4.7 us

profile of v3, /device:TPU:0, one launch (start us, length us, event | category | flops | bytes accessed | tf_op | source)
XLA Modules:
  0.0 108.1 jit_solution(8254165682868962886)
XLA Ops:
  0.0 103.2 %shard_map.64 = (bf16[16,256,1536]{2,1,0:T(8,128)(2,1)S(1)}, bf16[1536,1536]{1,0:T(8,128)(2,1)S(1)}, bf16[8,256,128]{2,1,0:T(8,128)(2,1)S(1)}, bf16[2,12,256,128...) custom-call(bf16[16,256,1536]{2,1,0:T(8,128)(2,1)} %x_hbm.1, s32[16,256]{1,0:T(8,128)} %pos_ref.1, ...), custom_call_target="tpu_custom_call" | custom-call | tf_op jit(solution)/shard_map/pallas_call | solution.py:394
  103.2 4.7 %shard_map.65 = bf16[16,256,1536]{2,1,0:T(8,128)(2,1)} custom-call(bf16[16,256,1536]{2,1,0:T(8,128)(2,1)S(1)} %get-tuple-element.10.xb, bf16[1536,1536]{1,0:T(8,128)(2,1)S(1)} %get-tuple-element.11.wo, bf16[8,256,128]{2,1,0:T(8,128)(2,1)S(1)} %get-tuple-element.12.kv_end, bf16[2,12,256,128]{3,2,1,0:T(8,128)(2,1)S(1)} %get-tuple-element.13.qb, ...), custom_call_target="tpu_custom_call" | custom-call | tf_op jit(solution)/shard_map/pallas_call | solution.py:420

commit v4 on v3

--- a/solution.py
+++ b/solution.py
@@ -16,7 +16,7 @@
 CP_SIZE = 4
 LAST = 2 * CP_SIZE - 1
 BLK = 128
-LEAD = 2
+LEAD = 3
 MESH = pl.DeviceIdType.MESH
 TURN = 2.0 ** 32
 SIN_COEF = [(-1) ** k * (2 * math.pi) ** (2 * k + 1) / math.factorial(2 * k + 1) for k in range(7)]
@@ -55,27 +55,27 @@
     return (wide * cos_tab + pltpu.roll(wide, HALF_DIM, 1) * sin_tab).astype(jnp.bfloat16)
 
 
-def attend(kv_row, row_of, q_row, o_row, sb, group, dev, groups, fill):
+def attend(kv_row, row_of, q_row, o_row, o_col, sb, dev, fill):
     wide = (BLK, 2 * BLK)
     tri = lax.broadcasted_iota(jnp.int32, wide, 0) <= lax.rem(lax.broadcasted_iota(jnp.int32, wide, 1), BLK)
-    units = [(half, g, h) for half in (1, 0) for g in groups for h in range(g * group, (g + 1) * group, 2)]
+    units = [(half, h) for half in (1, 0) for h in range(0, q_row.shape[0], 2)]
 
     def spans(half):
         n_blk = LAST - dev + 1 if half else dev + 1
         return n_blk, n_blk * BLK, slice(half * BLK, (half + 1) * BLK)
 
     starts, at = [], 0
-    for half, _, _ in units:
+    for half, _ in units:
         need = spans(half)[1]
         at = 0 if at + need > sb.shape[0] else at
         starts.append(at)
         at += need
 
     def score(k):
-        half, g, h = units[k]
+        half, h = units[k]
         n_blk, n_key, toks_at = spans(half)
         base = starts[k]
-        keys = kv_row[0:n_blk, row_of(g):row_of(g) + BLK, :].reshape(n_key, HEAD_DIM)
+        keys = kv_row[0:n_blk, row_of:row_of + BLK, :].reshape(n_key, HEAD_DIM)
         scores = nt_dot(keys, q_row[h:h + 2, toks_at, :].reshape(2 * BLK, HEAD_DIM))
         diag = jnp.where(tri, scores[n_key - BLK:], MASK_FILL)
         sb[base + n_key - BLK:base + n_key, :] = diag
@@ -86,15 +86,15 @@
         return top
 
     def weigh(k, top):
-        half, g, h = units[k]
+        half, h = units[k]
         n_blk, n_key, toks_at = spans(half)
         exp_w = jnp.exp2((sb[starts[k]:starts[k] + n_key, :] - top) * EXP_SCALE)
         inv = 1.0 / jnp.sum(exp_w, axis=0, keepdims=True)
-        lo = row_of(g) + BLK
+        lo = row_of + BLK
         vals = jnp.concatenate([kv_row[i, lo:lo + HEAD_DIM, :] for i in range(n_blk)], axis=1)
         out = (jnp.dot(vals, exp_w.astype(jnp.bfloat16), preferred_element_type=jnp.float32) * inv).T.astype(jnp.bfloat16)
         for i in range(2):
-            o_row[toks_at, (h + i) * HEAD_DIM:(h + i + 1) * HEAD_DIM] = out[i * BLK:(i + 1) * BLK]
+            o_row[toks_at, o_col + (h + i) * HEAD_DIM:o_col + (h + i + 1) * HEAD_DIM] = out[i * BLK:(i + 1) * BLK]
 
     count = len(units)
     tops = [score(k) for k in range(LEAD)]
@@ -105,14 +105,15 @@
         fill(k, count)
 
 
-def main_kernel(x_hbm, pos_ref, wq_hbm, wk_hbm, wv_hbm, wo_hbm, xb, wo, kv_end, qb, ob,
-                wq, wk, wv, kv, sb, high_b, low_b, cos_b, sin_b,
+def main_kernel(x_hbm, pos_ref, wq_hbm, wk_hbm, wv_hbm, wo_hbm, xb, wo, kv_end, q_tail, o_head,
+                wq, wk, wv, kv, q_head, q_next, o_full, sb, high_b, low_b, cos_b, sin_b,
                 xsem, wsem, ici_s, ici_r, sib_s, sib_r, fwd_s, fwd_r):
     rows, toks, width = xb.shape
     kv_cols = wk.shape[1]
     kv_heads = kv_cols // HEAD_DIM
     q_heads = wq.shape[1] // HEAD_DIM
     group = q_heads // kv_heads
+    head_cols = group * HEAD_DIM
     end = rows - 1
     me = lax.axis_index("cp")
     chip = me // 2
@@ -144,30 +145,29 @@
     def row_at(g):
         return g * (BLK + HEAD_DIM)
 
-    def remote(b, idx, half, send, recv, dev, head=None):
-        ref = kv.at[b, idx] if head is None else kv.at[b, idx, row_at(head):row_at(head + 1)]
-        sem = b if head is None else b + head
-        return pltpu.make_async_remote_copy(src_ref=ref, dst_ref=ref, send_sem=send.at[half, sem], recv_sem=recv.at[half, sem], device_id={"cp": dev}, device_id_type=MESH)
-
-    def send_link(b, head=None):
-        remote(b, me, 0, ici_s, ici_r, par, head).start()
-
-        @pl.when(chip == 1)
-        def _():
-            remote(b, LAST - me, 1, ici_s, ici_r, par, head).start()
-
-    def send_sib(b):
-        remote(b, me, 0, sib_s, sib_r, sib).start()
+    def remote(b, idx, half, send, recv, dev, head):
+        ref = kv.at[b, idx, row_at(head):row_at(head + 1)]
+        return pltpu.make_async_remote_copy(src_ref=ref, dst_ref=ref, send_sem=send.at[half, head, b], recv_sem=recv.at[half, head, b], device_id={"cp": dev}, device_id_type=MESH)
+
+    def sib_copy(b, idx, half):
+        ref = kv.at[b, idx]
+        return pltpu.make_async_remote_copy(src_ref=ref, dst_ref=ref, send_sem=sib_s.at[half, b], recv_sem=sib_r.at[half, b], device_id={"cp": sib}, device_id_type=MESH)
+
+    def send_row(b):
+        for head in range(kv_heads):
+            remote(b, me, 0, ici_s, ici_r, par, head).start()
+
+            @pl.when(chip == 1)
+            def _():
+                remote(b, LAST - me, 1, ici_s, ici_r, par, head).start()
+
+        sib_copy(b, me, 0).start()
 
         @pl.when(core == 1)
         def _():
-            remote(b, LAST - me, 1, sib_s, sib_r, sib).start()
-
-    def send_row(b):
-        send_link(b)
-        send_sib(b)
-
-    def relay(b, head=None):
+            sib_copy(b, LAST - me, 1).start()
+
+    def relay(b, head):
         remote(b, par, 0, ici_s, ici_r, par, head).wait_recv()
         remote(b, par, 0, fwd_s, fwd_r, sib, head).start()
 
@@ -177,13 +177,13 @@
             remote(b, LAST - par, 1, fwd_s, fwd_r, sib, head).start()
 
     def wait_sib(b):
-        remote(b, sib, 0, sib_s, sib_r, sib).wait_recv()
+        sib_copy(b, sib, 0).wait_recv()
 
         @pl.when(core == 0)
         def _():
-            remote(b, LAST - sib, 1, sib_s, sib_r, sib).wait_recv()
-
-    def wait_relay(b, head=None):
+            sib_copy(b, LAST - sib, 1).wait_recv()
+
+    def wait_relay(b, head):
         remote(b, dia, 0, fwd_s, fwd_r, sib, head).wait_recv()
 
         @pl.when(chip == 0)
@@ -213,21 +213,18 @@
                 kv[b, idx, at:at + BLK, :] = rope_head(k_row[lo:lo + BLK, cols], cos_tab[lo:lo + BLK], sin_tab[lo:lo + BLK])
                 kv[b, idx, at + BLK:at + BLK + HEAD_DIM, :] = v_row[lo:lo + BLK, cols].T.astype(jnp.bfloat16)
 
-    def make_q(b, slot):
-        x_row = xb[b]
+    def q_tile(b, n):
         cos_tab, sin_tab = cos_b[b], sin_b[b]
-        for n in range(0, q_heads, 2):
-            pair = jnp.dot(x_row, wq[:, n * HEAD_DIM:(n + 2) * HEAD_DIM], preferred_element_type=jnp.float32).astype(jnp.bfloat16)
-            for i in range(2):
-                qb[slot, n + i] = rope_head(pair[:, i * HEAD_DIM:(i + 1) * HEAD_DIM], cos_tab, sin_tab)
+        pair = jnp.dot(xb[b], wq[:, n * HEAD_DIM:(n + 2) * HEAD_DIM], preferred_element_type=jnp.float32).astype(jnp.bfloat16)
+        for i in range(2):
+            ref, h = (q_head, n + i) if n < group else (q_next, n + i - group)
+            ref[h] = rope_head(pair[:, i * HEAD_DIM:(i + 1) * HEAD_DIM], cos_tab, sin_tab)
 
     out_tiles = width // (2 * HEAD_DIM)
 
-    def out_tile(b, slot, n, keep):
+    def out_tile(b, n, keep):
         cols = slice(n * 2 * HEAD_DIM, (n + 1) * 2 * HEAD_DIM)
-        y_part = jnp.dot(ob[slot], wo[:, cols], preferred_element_type=jnp.float32)
-        if keep is not None:
-            y_part = jnp.where(keep, y_part, 0.0)
+        y_part = jnp.where(keep, jnp.dot(o_full[...], wo[:, cols], preferred_element_type=jnp.float32), 0.0)
         xb[b, :, cols] = (xb[b, :, cols].astype(jnp.float32) + y_part).astype(jnp.bfloat16)
 
     for b in range(1, 5):
@@ -270,105 +267,95 @@
     x_copy(end).wait()
     w_copies[2].wait()
     make_kv(end)
-    make_q(0, 0)
-    send_link(end, 0)
-    send_link(end, 1)
-    send_sib(end)
+    for n in range(0, q_heads, 2):
+        q_tile(0, n)
+    send_row(end)
     w_copies[3].wait()
 
+    def spread(step, steps):
+        def fill(k, count):
+            for n in range(k * steps // count, (k + 1) * steps // count):
+                step(n)
+        return fill
+
     def row_step(b, _):
-        slot = lax.rem(b, 2)
-        relay(b)
-        make_q(b + 1, 1 - slot)
+        b_old = jnp.maximum(b - 1, 0)
+        relay(b, 0)
+
+        @pl.when(b > 0)
+        def _():
+            wait_relay(b_old, 1)
+
+        for dev in range(CP_SIZE):
+            @pl.when((me == dev) & (b > 0))
+            def _():
+                o_full[:, :head_cols] = o_head[...]
+                attend(kv.at[b_old], row_at(1), q_tail, o_full, head_cols, sb, dev, spread(lambda n: q_tile(b, 2 * n), q_heads // 2))
+
         wait_sib(b)
-        wait_relay(b)
-
-        def fill(k, count):
-            if (k + 1) * out_tiles // count > k * out_tiles // count:
-                out_tile(jnp.maximum(b - 1, 0), 1 - slot, k * out_tiles // count, b > 0)
-
+        wait_relay(b, 0)
+        relay(b, 1)
         for dev in range(CP_SIZE):
             @pl.when(me == dev)
             def _():
-                attend(kv.at[b], row_at, qb.at[slot], ob.at[slot], sb, group, dev, range(kv_heads), fill)
+                q_tail[...] = q_next[...]
+                attend(kv.at[b], row_at(0), q_head, o_head, 0, sb, dev, spread(lambda n: out_tile(b_old, n, b > 0), out_tiles))
 
         return _
 
-    lax.fori_loop(0, end, row_step, None)
-    slot = end % 2
-    relay(end, 0)
-    for n in range(out_tiles):
-        out_tile(end - 1, 1 - slot, n, None)
-    wait_sib(end)
-    wait_relay(end, 0)
-    for dev in range(CP_SIZE):
-        @pl.when(me == dev)
-        def _():
-            attend(kv.at[end], row_at, qb.at[slot], ob.at[slot], sb, group, dev, range(kv_heads - 1), lambda k, count: None)
-
-    relay(end, 1)
+    lax.fori_loop(0, rows, row_step, None)
     wait_relay(end, 1)
     kv_end[...] = kv[end, :, row_at(kv_heads - 1):row_at(kv_heads), :]
 
-    def drain(b, head):
-        remote(b, me, 0, ici_s, ici_r, par, head).wait_send()
-        remote(b, par, 0, fwd_s, fwd_r, sib, head).wait_send()
-
-        @pl.when(chip == 1)
-        def _():
-            remote(b, LAST - me, 1, ici_s, ici_r, par, head).wait_send()
-
-        @pl.when(chip == 0)
-        def _():
-            remote(b, LAST - par, 1, fwd_s, fwd_r, sib, head).wait_send()
-
-    def drain_sib(b):
-        remote(b, me, 0, sib_s, sib_r, sib).wait_send()
+    def drain_row(b, _):
+        for head in range(kv_heads):
+            remote(b, me, 0, ici_s, ici_r, par, head).wait_send()
+            remote(b, par, 0, fwd_s, fwd_r, sib, head).wait_send()
+
+            @pl.when(chip == 1)
+            def _():
+                remote(b, LAST - me, 1, ici_s, ici_r, par, head).wait_send()
+
+            @pl.when(chip == 0)
+            def _():
+                remote(b, LAST - par, 1, fwd_s, fwd_r, sib, head).wait_send()
+
+        sib_copy(b, me, 0).wait_send()
 
         @pl.when(core == 1)
         def _():
-            remote(b, LAST - me, 1, sib_s, sib_r, sib).wait_send()
-
-    def drain_row(b, _):
-        drain(b, None)
-        drain_sib(b)
+            sib_copy(b, LAST - me, 1).wait_send()
+
         return _
 
-    lax.fori_loop(0, end, drain_row, None)
-    drain(end, 0)
-    drain(end, 1)
-    drain_sib(end)
-
-
-def end_kernel(xb, wo, kv_end, qb, ob, y_hbm, sb, o_new, acc, y_row, sem):
+    lax.fori_loop(0, rows, drain_row, None)
+
+
+def end_kernel(xb, wo, kv_end, q_tail, o_head, y_hbm, sb, o_tail, acc, y_row, sem):
     rows, toks, width = xb.shape
-    q_heads = qb.shape[1]
-    kv_heads = 2
-    group = q_heads // kv_heads
     end = rows - 1
-    slot = end % 2
     me = lax.axis_index("cp")
     copies = [pltpu.make_async_copy(xb.at[b], y_hbm.at[b], sem.at[b]) for b in range(end)]
     for copy in copies:
         copy.start()
-    old = (kv_heads - 1) * group * HEAD_DIM
+    old = o_head.shape[1]
     tile = 2 * HEAD_DIM
     out_tiles = width // tile
 
     def fill(k, count):
         for n in range(k * out_tiles // count, (k + 1) * out_tiles // count):
             cols = slice(n * tile, (n + 1) * tile)
-            acc[:, cols] = xb[end, :, cols].astype(jnp.float32) + jnp.dot(ob[slot, :, :old], wo[:old, cols], preferred_element_type=jnp.float32)
+            acc[:, cols] = xb[end, :, cols].astype(jnp.float32) + jnp.dot(o_head[...], wo[:old, cols], preferred_element_type=jnp.float32)
 
     for dev in range(CP_SIZE):
         @pl.when(me == dev)
         def _():
-            attend(kv_end, lambda g: 0, qb.at[slot], o_new, sb, group, dev, (kv_heads - 1,), fill)
+            attend(kv_end, 0, q_tail, o_tail, 0, sb, dev, fill)
 
     last_copies = []
     for n in range(out_tiles):
         cols = slice(n * tile, (n + 1) * tile)
-        y_row[:, cols] = (acc[:, cols] + jnp.dot(o_new[:, old:], wo[old:, cols], preferred_element_type=jnp.float32)).astype(jnp.bfloat16)
+        y_row[:, cols] = (acc[:, cols] + jnp.dot(o_tail[...], wo[old:, cols], preferred_element_type=jnp.float32)).astype(jnp.bfloat16)
         if n % 2:
             span = slice((n - 1) * tile, (n + 1) * tile)
             last_copies.append(pltpu.make_async_copy(y_row.at[:, span], y_hbm.at[end, :, span], sem.at[end + n // 2]))
@@ -385,11 +372,12 @@
     def local_block(x_loc, pos_loc, w_query, w_key, w_value, w_out):
         rows, toks, width = x_loc.shape
         q_cols, kv_cols = w_query.shape[1], w_key.shape[1]
-        q_heads = q_cols // HEAD_DIM
+        group = q_cols // kv_cols
         any_spec = pl.BlockSpec(memory_space=pl.ANY)
         vmem_spec = pl.BlockSpec(memory_space=pltpu.VMEM)
         bf16, f32 = jnp.bfloat16, jnp.float32
-        pair_sem = pltpu.SemaphoreType.DMA((2, rows + 1))
+        pair_sem = pltpu.SemaphoreType.DMA((2, rows))
+        head_sem = pltpu.SemaphoreType.DMA((2, kv_cols // HEAD_DIM, rows))
         row_sem = pltpu.SemaphoreType.DMA((rows,))
         kept = pl.pallas_call(
             main_kernel,
@@ -397,8 +385,8 @@
                 pltpu.VMEM(x_loc.shape, bf16),
                 pltpu.VMEM((q_cols, width), bf16),
                 pltpu.VMEM((2 * CP_SIZE, BLK + HEAD_DIM, BLK), bf16),
-                pltpu.VMEM((2, q_heads, toks, HEAD_DIM), bf16),
-                pltpu.VMEM((2, toks, q_cols), bf16),
+                pltpu.VMEM((group, toks, HEAD_DIM), bf16),
+                pltpu.VMEM((toks, group * HEAD_DIM), bf16),
             ],
             in_specs=[any_spec, vmem_spec] + [any_spec] * 4,
             out_specs=[vmem_spec] * 5,
@@ -407,13 +395,16 @@
                 pltpu.VMEM((width, kv_cols), bf16),
                 pltpu.VMEM((width, kv_cols), bf16),
                 pltpu.VMEM((rows, 2 * CP_SIZE, 2 * kv_cols, BLK), bf16),
+                pltpu.VMEM((group, toks, HEAD_DIM), bf16),
+                pltpu.VMEM((group, toks, HEAD_DIM), bf16),
+                pltpu.VMEM((toks, q_cols), bf16),
                 pltpu.VMEM((4 * CP_SIZE * toks, 2 * BLK), f32),
                 pltpu.VMEM((HALF_DIM, toks), jnp.int32),
                 pltpu.VMEM((HALF_DIM, toks), f32),
                 pltpu.VMEM((rows, toks, HEAD_DIM), f32),
                 pltpu.VMEM((rows, toks, HEAD_DIM), f32),
                 row_sem, pltpu.SemaphoreType.DMA((4,)),
-                pair_sem, pair_sem, pair_sem, pair_sem, pair_sem, pair_sem,
+                head_sem, head_sem, pair_sem, pair_sem, head_sem, head_sem,
             ],
             compiler_params=pltpu.CompilerParams(collective_id=0, has_side_effects=True, vmem_limit_bytes=36 * 1024 * 1024),
         )(x_loc, pos_loc, w_query, w_key, w_value, w_out)
@@ -424,7 +415,7 @@
             out_specs=any_spec,
             scratch_shapes=[
                 pltpu.VMEM((4 * CP_SIZE * toks, 2 * BLK), f32),
-                pltpu.VMEM((toks, q_cols), bf16),
+                pltpu.VMEM((toks, group * HEAD_DIM), bf16),
                 pltpu.VMEM((toks, width), f32),
                 pltpu.VMEM((toks, width), bf16),
                 pltpu.SemaphoreType.DMA((rows + 2,)),

time: 108 us -> 108 us (level)
  no operation moved by 1% of the time
where the time goes in v4:
time: 108 us
  Pallas kernels  107 us (99%)
    pallas_call x1, Pallas kernels, local_block(): pl.pallas_call(main_kernel, out_shape=[pltpu.VMEM(x_loc.shape, bf16), plt...  103 us
    pallas_call x1, Pallas kernels, local_block(): pl.pallas_call(end_kernel, out_shape=jax.ShapeDtypeStruct(x_loc.shape, bf...  4.7 us

profile of v4, /device:TPU:0, one launch (start us, length us, event | category | flops | bytes accessed | tf_op | source)
XLA Modules:
  0.0 108.2 jit_solution(15423073192663210648)
XLA Ops:
  0.0 0.0 copy-start
  0.0 0.7 copy-done
  0.7 102.6 %shard_map.64 = (bf16[16,256,1536]{2,1,0:T(8,128)(2,1)S(1)}, bf16[1536,1536]{1,0:T(8,128)(2,1)S(1)}, bf16[8,256,128]{2,1,0:T(8,128)(2,1)S(1)}, bf16[6,256,128]{2,1,0:T(8,128)(2,1)S(1)}, bf16[256,768]{1,0:T(8,128)(2,1)S(1)}) custom-call(bf16[16,256,1536]{2,1,0:T(8,128)(2,1)} %x_hbm.1, s32[16,256]{1,0:T(8,128)S(1)} %copy-done, bf16[1536,1536]{1,0:T(8,128)(2,1)} %wq_hbm.1, ...), custom_call_target="tpu_custom_call" | custom-call | tf_op jit(solution)/shard_map/pallas_call | solution.py:382
  103.3 4.7 %shard_map.65 = bf16[16,256,1536]{2,1,0:T(8,128)(2,1)} custom-call(bf16[16,256,1536]{2,1,0:T(8,128)(2,1)S(1)} %get-tuple-element.10.xb, bf16[1536,1536]{1,0:T(8,128)(2,1)S(1)} %get-tuple-element.11.wo, bf16[8,256,128]{2,1,0:T(8,128)(2,1)S(1)} %get-tuple-element.12.kv_end, bf16[6,256,128]{2,1,0:T(8,128)(2,1)S(1)} %get-tuple-element.13.q_tail, ...), custom_call_target="tpu_custom_call" | custom-call | tf_op jit(solution)/shard_map/pallas_call | solution.py:411
Async XLA Ops:
  0.0 0.7 copy-start

commit v5 on v4

--- a/solution.py
+++ b/solution.py
@@ -105,8 +105,8 @@
         fill(k, count)
 
 
-def main_kernel(x_hbm, pos_ref, wq_hbm, wk_hbm, wv_hbm, wo_hbm, xb, wo, kv_end, q_tail, o_head,
-                wq, wk, wv, kv, q_head, q_next, o_full, sb, high_b, low_b, cos_b, sin_b,
+def main_kernel(x_hbm, pos_hbm, wq_hbm, wk_hbm, wv_hbm, wo_hbm, xb, wo, kv_end, q_tail, o_head,
+                wq, wk, wv, kv, q_head, q_next, o_full, sb, pos_ref, high_b, low_b, cos_b, sin_b,
                 xsem, wsem, ici_s, ici_r, sib_s, sib_r, fwd_s, fwd_r):
     rows, toks, width = xb.shape
     kv_cols = wk.shape[1]
@@ -122,7 +122,7 @@
     par = (1 - chip) * 2 + core
     dia = (1 - chip) * 2 + (1 - core)
 
-    w_copies = [pltpu.make_async_copy(src, dst, wsem.at[i]) for i, (src, dst) in enumerate(((wk_hbm, wk), (wv_hbm, wv), (wq_hbm, wq), (wo_hbm, wo)))]
+    w_copies = [pltpu.make_async_copy(src, dst, wsem.at[i]) for i, (src, dst) in enumerate(((wk_hbm, wk), (wv_hbm, wv), (wq_hbm, wq), (wo_hbm, wo), (pos_hbm, pos_ref)))]
 
     def x_copy(b):
         return pltpu.make_async_copy(x_hbm.at[b], xb.at[b], xsem.at[b])
@@ -134,61 +134,58 @@
 
     w_copies[0].start()
     x_copy(0).start()
+    w_copies[4].start()
     w_copies[1].start()
-    high_b[...], low_b[...] = turn_tables(toks)
-
     barrier = pltpu.get_barrier_semaphore()
     for other in (sib, par):
         pl.semaphore_signal(barrier, inc=1, device_id={"cp": other}, device_id_type=MESH)
-    pl.semaphore_wait(barrier, 2)
+    high_b[...], low_b[...] = turn_tables(toks)
 
     def row_at(g):
         return g * (BLK + HEAD_DIM)
 
-    def remote(b, idx, half, send, recv, dev, head):
-        ref = kv.at[b, idx, row_at(head):row_at(head + 1)]
-        return pltpu.make_async_remote_copy(src_ref=ref, dst_ref=ref, send_sem=send.at[half, head, b], recv_sem=recv.at[half, head, b], device_id={"cp": dev}, device_id_type=MESH)
-
-    def sib_copy(b, idx, half):
-        ref = kv.at[b, idx]
-        return pltpu.make_async_remote_copy(src_ref=ref, dst_ref=ref, send_sem=sib_s.at[half, b], recv_sem=sib_r.at[half, b], device_id={"cp": sib}, device_id_type=MESH)
+    def piece(b, idx, head):
+        return kv.at[b, idx] if head is None else kv.at[b, idx, row_at(head):row_at(head + 1)]
+
+    def remote(ref, send, recv, dev):
+        return pltpu.make_async_remote_copy(src_ref=ref, dst_ref=ref, send_sem=send, recv_sem=recv, device_id={"cp": dev}, device_id_type=MESH)
+
+    def either(twin, act):
+        @pl.when(twin)
+        def _():
+            act(2)
+
+        @pl.when(jnp.logical_not(twin))
+        def _():
+            act(1)
 
     def send_row(b):
         for head in range(kv_heads):
-            remote(b, me, 0, ici_s, ici_r, par, head).start()
+            remote(piece(b, me, head), ici_s, ici_r.at[head, b], par).start()
 
             @pl.when(chip == 1)
             def _():
-                remote(b, LAST - me, 1, ici_s, ici_r, par, head).start()
-
-        sib_copy(b, me, 0).start()
+                remote(piece(b, LAST - me, head), ici_s, ici_r.at[head, b], par).start()
+
+        remote(piece(b, me, None), sib_s, sib_r.at[b], sib).start()
 
         @pl.when(core == 1)
         def _():
-            sib_copy(b, LAST - me, 1).start()
+            remote(piece(b, LAST - me, None), sib_s, sib_r.at[b], sib).start()
 
     def relay(b, head):
-        remote(b, par, 0, ici_s, ici_r, par, head).wait_recv()
-        remote(b, par, 0, fwd_s, fwd_r, sib, head).start()
+        either(chip == 0, lambda n: remote(piece(b, slice(0, n), head), ici_s, ici_r.at[head, b], par).wait_recv())
+        remote(piece(b, par, head), fwd_s, fwd_r.at[head, b], sib).start()
 
         @pl.when(chip == 0)
         def _():
-            remote(b, LAST - par, 1, ici_s, ici_r, par, head).wait_recv()
-            remote(b, LAST - par, 1, fwd_s, fwd_r, sib, head).start()
+            remote(piece(b, LAST - par, head), fwd_s, fwd_r.at[head, b], sib).start()
 
     def wait_sib(b):
-        sib_copy(b, sib, 0).wait_recv()
-
-        @pl.when(core == 0)
-        def _():
-            sib_copy(b, LAST - sib, 1).wait_recv()
+        either(core == 0, lambda n: remote(piece(b, slice(0, n), None), sib_s, sib_r.at[b], sib).wait_recv())
 
     def wait_relay(b, head):
-        remote(b, dia, 0, fwd_s, fwd_r, sib, head).wait_recv()
-
-        @pl.when(chip == 0)
-        def _():
-            remote(b, LAST - dia, 1, fwd_s, fwd_r, sib, head).wait_recv()
+        either(chip == 0, lambda n: remote(piece(b, slice(0, n), head), fwd_s, fwd_r.at[head, b], sib).wait_recv())
 
     def make_kv(b):
         pos = pos_ref[pl.ds(b, 1), :]
@@ -227,12 +224,14 @@
         y_part = jnp.where(keep, jnp.dot(o_full[...], wo[:, cols], preferred_element_type=jnp.float32), 0.0)
         xb[b, :, cols] = (xb[b, :, cols].astype(jnp.float32) + y_part).astype(jnp.bfloat16)
 
+    for copy in (w_copies[4], w_copies[0], x_copy(0)):
+        copy.wait()
     for b in range(1, 5):
         x_copy(b).start()
-    w_copies[0].wait()
-    x_copy(0).wait()
     w_copies[1].wait()
     make_kv(0)
+    pl.semaphore_wait(barrier, 2)
+    send_row(0)
 
     def kv_step(i, _):
         at = 2 * i + 1
@@ -242,8 +241,8 @@
         @pl.when(i > 0)
         def _():
             send_row(at - 2)
-
-        send_row(at - 1)
+            send_row(at - 1)
+
         for b in (at + 4, at + 5):
             @pl.when(b < rows)
             def _():
@@ -307,28 +306,9 @@
     wait_relay(end, 1)
     kv_end[...] = kv[end, :, row_at(kv_heads - 1):row_at(kv_heads), :]
 
-    def drain_row(b, _):
-        for head in range(kv_heads):
-            remote(b, me, 0, ici_s, ici_r, par, head).wait_send()
-            remote(b, par, 0, fwd_s, fwd_r, sib, head).wait_send()
-
-            @pl.when(chip == 1)
-            def _():
-                remote(b, LAST - me, 1, ici_s, ici_r, par, head).wait_send()
-
-            @pl.when(chip == 0)
-            def _():
-                remote(b, LAST - par, 1, fwd_s, fwd_r, sib, head).wait_send()
-
-        sib_copy(b, me, 0).wait_send()
-
-        @pl.when(core == 1)
-        def _():
-            sib_copy(b, LAST - me, 1).wait_send()
-
-        return _
-
-    lax.fori_loop(0, rows, drain_row, None)
+    either(chip == 1, lambda n: remote(kv.at[:, 0:n], ici_s, ici_r.at[0, 0], par).wait_send())
+    either(chip == 0, lambda n: remote(kv.at[:, 0:n], fwd_s, fwd_r.at[0, 0], sib).wait_send())
+    either(core == 1, lambda n: remote(kv.at[:, 0:n], sib_s, sib_r.at[0], sib).wait_send())
 
 
 def end_kernel(xb, wo, kv_end, q_tail, o_head, y_hbm, sb, o_tail, acc, y_row, sem):
@@ -376,8 +356,8 @@
         any_spec = pl.BlockSpec(memory_space=pl.ANY)
         vmem_spec = pl.BlockSpec(memory_space=pltpu.VMEM)
         bf16, f32 = jnp.bfloat16, jnp.float32
-        pair_sem = pltpu.SemaphoreType.DMA((2, rows))
-        head_sem = pltpu.SemaphoreType.DMA((2, kv_cols // HEAD_DIM, rows))
+        one_sem = pltpu.SemaphoreType.DMA
+        head_sem = pltpu.SemaphoreType.DMA((kv_cols // HEAD_DIM, rows))
         row_sem = pltpu.SemaphoreType.DMA((rows,))
         kept = pl.pallas_call(
             main_kernel,
@@ -388,7 +368,7 @@
                 pltpu.VMEM((group, toks, HEAD_DIM), bf16),
                 pltpu.VMEM((toks, group * HEAD_DIM), bf16),
             ],
-            in_specs=[any_spec, vmem_spec] + [any_spec] * 4,
+            in_specs=[any_spec] * 6,
             out_specs=[vmem_spec] * 5,
             scratch_shapes=[
                 pltpu.VMEM((width, q_cols), bf16),
@@ -399,14 +379,15 @@
                 pltpu.VMEM((group, toks, HEAD_DIM), bf16),
                 pltpu.VMEM((toks, q_cols), bf16),
                 pltpu.VMEM((4 * CP_SIZE * toks, 2 * BLK), f32),
+                pltpu.VMEM((rows, toks), jnp.int32),
                 pltpu.VMEM((HALF_DIM, toks), jnp.int32),
                 pltpu.VMEM((HALF_DIM, toks), f32),
                 pltpu.VMEM((rows, toks, HEAD_DIM), f32),
                 pltpu.VMEM((rows, toks, HEAD_DIM), f32),
-                row_sem, pltpu.SemaphoreType.DMA((4,)),
-                head_sem, head_sem, pair_sem, pair_sem, head_sem, head_sem,
+                row_sem, pltpu.SemaphoreType.DMA((5,)),
+                one_sem, head_sem, one_sem, row_sem, one_sem, head_sem,
             ],
-            compiler_params=pltpu.CompilerParams(collective_id=0, has_side_effects=True, vmem_limit_bytes=36 * 1024 * 1024),
+            compiler_params=pltpu.CompilerParams(collective_id=0, has_side_effects=True, vmem_limit_bytes=43 * 1024 * 1024),
         )(x_loc, pos_loc, w_query, w_key, w_value, w_out)
         return pl.pallas_call(
             end_kernel,

time: 108 us -> 105 us (0.972)
  Pallas kernels: 107 us -> 105 us
    pallas_call x1, Pallas kernels: 103 us -> 100 us  [local_block(): pl.pallas_call(main_kernel, out_shape=[pltpu.VMEM(x_loc.shape, bf16), plt...]
where the time goes in v5:
time: 105 us
  Pallas kernels  105 us (100%)
    pallas_call x1, Pallas kernels, local_block(): pl.pallas_call(main_kernel, out_shape=[pltpu.VMEM(x_loc.shape, bf16), plt...  100 us
    pallas_call x1, Pallas kernels, local_block(): pl.pallas_call(end_kernel, out_shape=jax.ShapeDtypeStruct(x_loc.shape, bf...  4.7 us

profile of v5, /device:TPU:0, one launch (start us, length us, event | category | flops | bytes accessed | tf_op | source)
XLA Modules:
  0.0 105.1 jit_solution(743827131932331747)
XLA Ops:
  0.0 100.2 %shard_map.64 = (bf16[16,256,1536]{2,1,0:T(8,128)(2,1)S(1)}, bf16[1536,1536]{1,0:T(8,128)(2,1)S(1)}, bf16[8,256,128]{2,1,0:T(8,128)(2,1)S(1)}, bf16[6,256,128]{2,1,0:T(8,128)(2,1)S(1)}, bf16[256,768]{1,0:T(8,128)(2,1)S(1)}) custom-call(bf16[16,256,1536]{2,1,0:T(8,128)(2,1)} %x_hbm.1, s32[16,256]{1,0:T(8,128)} %pos_hbm.1, bf16[1536,1536]{1,0:T(8,128)(2,1)} %wq_hbm.1, ...), custom_call_target="tpu_custom_call" | custom-call | tf_op jit(solution)/shard_map/pallas_call | solution.py:362
  100.2 4.7 %shard_map.65 = bf16[16,256,1536]{2,1,0:T(8,128)(2,1)} custom-call(bf16[16,256,1536]{2,1,0:T(8,128)(2,1)S(1)} %get-tuple-element.10.xb, bf16[1536,1536]{1,0:T(8,128)(2,1)S(1)} %get-tuple-element.11.wo, bf16[8,256,128]{2,1,0:T(8,128)(2,1)S(1)} %get-tuple-element.12.kv_end, bf16[6,256,128]{2,1,0:T(8,128)(2,1)S(1)} %get-tuple-element.13.q_tail, ...), custom_call_target="tpu_custom_call" | custom-call | tf_op jit(solution)/shard_map/pallas_call | solution.py:392

commit v6 on v5

--- a/solution.py
+++ b/solution.py
@@ -105,8 +105,8 @@
         fill(k, count)
 
 
-def main_kernel(x_hbm, pos_hbm, wq_hbm, wk_hbm, wv_hbm, wo_hbm, xb, wo, kv_end, q_tail, o_head,
-                wq, wk, wv, kv, q_head, q_next, o_full, sb, pos_ref, high_b, low_b, cos_b, sin_b,
+def main_kernel(x_hbm, pos_hbm, wq_hbm, wk_hbm, wv_hbm, wo_hbm, xb, wo, kv_end, q_head, q_next, o_full,
+                wq, wk, wv, kv, q_tail, o_head, sb, pos_ref, high_b, low_b, cos_b, sin_b,
                 xsem, wsem, ici_s, ici_r, sib_s, sib_r, fwd_s, fwd_r):
     rows, toks, width = xb.shape
     kv_cols = wk.shape[1]
@@ -295,7 +295,7 @@
         wait_relay(b, 0)
         relay(b, 1)
         for dev in range(CP_SIZE):
-            @pl.when(me == dev)
+            @pl.when((me == dev) & (b < end))
             def _():
                 q_tail[...] = q_next[...]
                 attend(kv.at[b], row_at(0), q_head, o_head, 0, sb, dev, spread(lambda n: out_tile(b_old, n, b > 0), out_tiles))
@@ -303,44 +303,55 @@
         return _
 
     lax.fori_loop(0, rows, row_step, None)
+    kv_end[:, :row_at(1), :] = kv[end, :, :row_at(1), :]
     wait_relay(end, 1)
-    kv_end[...] = kv[end, :, row_at(kv_heads - 1):row_at(kv_heads), :]
+    kv_end[:, row_at(1):, :] = kv[end, :, row_at(1):, :]
 
     either(chip == 1, lambda n: remote(kv.at[:, 0:n], ici_s, ici_r.at[0, 0], par).wait_send())
     either(chip == 0, lambda n: remote(kv.at[:, 0:n], fwd_s, fwd_r.at[0, 0], sib).wait_send())
     either(core == 1, lambda n: remote(kv.at[:, 0:n], sib_s, sib_r.at[0], sib).wait_send())
 
 
-def end_kernel(xb, wo, kv_end, q_tail, o_head, y_hbm, sb, o_tail, acc, y_row, sem):
+def end_kernel(xb, wo, kv_end, q_head, q_tail, o_full, y_hbm, sb, o_head, o_tail, acc, y_rows, sem):
     rows, toks, width = xb.shape
     end = rows - 1
     me = lax.axis_index("cp")
-    copies = [pltpu.make_async_copy(xb.at[b], y_hbm.at[b], sem.at[b]) for b in range(end)]
+    copies = [pltpu.make_async_copy(xb.at[b], y_hbm.at[b], sem.at[b]) for b in range(end - 1)]
     for copy in copies:
         copy.start()
     old = o_head.shape[1]
     tile = 2 * HEAD_DIM
     out_tiles = width // tile
 
-    def fill(k, count):
-        for n in range(k * out_tiles // count, (k + 1) * out_tiles // count):
-            cols = slice(n * tile, (n + 1) * tile)
-            acc[:, cols] = xb[end, :, cols].astype(jnp.float32) + jnp.dot(o_head[...], wo[:old, cols], preferred_element_type=jnp.float32)
+    def spread(step):
+        def fill(k, count):
+            for n in range(k * out_tiles // count, (k + 1) * out_tiles // count):
+                step(slice(n * tile, (n + 1) * tile))
+        return fill
+
+    def out_before(cols):
+        y_part = jnp.dot(o_full[...], wo[:, cols], preferred_element_type=jnp.float32)
+        y_rows[0, :, cols] = (xb[end - 1, :, cols].astype(jnp.float32) + y_part).astype(jnp.bfloat16)
+
+    def out_head(cols):
+        acc[:, cols] = xb[end, :, cols].astype(jnp.float32) + jnp.dot(o_head[...], wo[:old, cols], preferred_element_type=jnp.float32)
 
     for dev in range(CP_SIZE):
         @pl.when(me == dev)
         def _():
-            attend(kv_end, 0, q_tail, o_tail, 0, sb, dev, fill)
-
-    last_copies = []
+            attend(kv_end, 0, q_head, o_head, 0, sb, dev, spread(out_before))
+            attend(kv_end, BLK + HEAD_DIM, q_tail, o_tail, 0, sb, dev, spread(out_head))
+
+    copies.append(pltpu.make_async_copy(y_rows.at[0], y_hbm.at[end - 1], sem.at[end - 1]))
+    copies[-1].start()
     for n in range(out_tiles):
         cols = slice(n * tile, (n + 1) * tile)
-        y_row[:, cols] = (acc[:, cols] + jnp.dot(o_tail[...], wo[old:, cols], preferred_element_type=jnp.float32)).astype(jnp.bfloat16)
+        y_rows[1, :, cols] = (acc[:, cols] + jnp.dot(o_tail[...], wo[old:, cols], preferred_element_type=jnp.float32)).astype(jnp.bfloat16)
         if n % 2:
             span = slice((n - 1) * tile, (n + 1) * tile)
-            last_copies.append(pltpu.make_async_copy(y_row.at[:, span], y_hbm.at[end, :, span], sem.at[end + n // 2]))
-            last_copies[-1].start()
-    for copy in copies + last_copies:
+            copies.append(pltpu.make_async_copy(y_rows.at[1, :, span], y_hbm.at[end, :, span], sem.at[end + n // 2]))
+            copies[-1].start()
+    for copy in copies:
         copy.wait()
 
 
@@ -364,20 +375,20 @@
             out_shape=[
                 pltpu.VMEM(x_loc.shape, bf16),
                 pltpu.VMEM((q_cols, width), bf16),
-                pltpu.VMEM((2 * CP_SIZE, BLK + HEAD_DIM, BLK), bf16),
+                pltpu.VMEM((2 * CP_SIZE, 2 * kv_cols, BLK), bf16),
                 pltpu.VMEM((group, toks, HEAD_DIM), bf16),
-                pltpu.VMEM((toks, group * HEAD_DIM), bf16),
+                pltpu.VMEM((group, toks, HEAD_DIM), bf16),
+                pltpu.VMEM((toks, q_cols), bf16),
             ],
             in_specs=[any_spec] * 6,
-            out_specs=[vmem_spec] * 5,
+            out_specs=[vmem_spec] * 6,
             scratch_shapes=[
                 pltpu.VMEM((width, q_cols), bf16),
                 pltpu.VMEM((width, kv_cols), bf16),
                 pltpu.VMEM((width, kv_cols), bf16),
                 pltpu.VMEM((rows, 2 * CP_SIZE, 2 * kv_cols, BLK), bf16),
                 pltpu.VMEM((group, toks, HEAD_DIM), bf16),
-                pltpu.VMEM((group, toks, HEAD_DIM), bf16),
-                pltpu.VMEM((toks, q_cols), bf16),
+                pltpu.VMEM((toks, group * HEAD_DIM), bf16),
                 pltpu.VMEM((4 * CP_SIZE * toks, 2 * BLK), f32),
                 pltpu.VMEM((rows, toks), jnp.int32),
                 pltpu.VMEM((HALF_DIM, toks), jnp.int32),
@@ -392,13 +403,14 @@
         return pl.pallas_call(
             end_kernel,
             out_shape=jax.ShapeDtypeStruct(x_loc.shape, bf16),
-            in_specs=[vmem_spec] * 5,
+            in_specs=[vmem_spec] * 6,
             out_specs=any_spec,
             scratch_shapes=[
                 pltpu.VMEM((4 * CP_SIZE * toks, 2 * BLK), f32),
                 pltpu.VMEM((toks, group * HEAD_DIM), bf16),
+                pltpu.VMEM((toks, group * HEAD_DIM), bf16),
                 pltpu.VMEM((toks, width), f32),
-                pltpu.VMEM((toks, width), bf16),
+                pltpu.VMEM((2, toks, width), bf16),
                 pltpu.SemaphoreType.DMA((rows + 2,)),
             ],
             compiler_params=pltpu.CompilerParams(vmem_limit_bytes=16 * 1024 * 1024),

time: 105 us -> 104 us (level)
    pallas_call x1, Pallas kernels: 100 us -> 98.6 us  [local_block(): pl.pallas_call(main_kernel, out_shape=[pltpu.VMEM(x_loc.shape, bf16), plt...]
where the time goes in v6:
time: 104 us
  Pallas kernels  104 us (100%)
    pallas_call x1, Pallas kernels, local_block(): pl.pallas_call(main_kernel, out_shape=[pltpu.VMEM(x_loc.shape, bf16), plt...  98.6 us
    pallas_call x1, Pallas kernels, local_block(): pl.pallas_call(end_kernel, out_shape=jax.ShapeDtypeStruct(x_loc.shape, bf...  5.53 us

profile of v6, /device:TPU:0, one launch (start us, length us, event | category | flops | bytes accessed | tf_op | source)
XLA Modules:
  0.0 104.4 jit_solution(12710659135714713638)
XLA Ops:
  0.0 98.6 %shard_map.64 = (bf16[16,256,1536]{2,1,0:T(8,128)(2,1)S(1)}, bf16[1536,1536]{1,0:T(8,128)(2,1)S(1)}, bf16[8,512,128]{2,1,0:T(8,128)(2,1)S(1)}, bf16[6,256,128]{2...) custom-call(bf16[16,256,1536]{2,1,0:T(8,128)(2,1)} %x_hbm.1, s32[16,256]{1,0:T(8,128)} %pos_hbm.1, ...), custom_call_target="tpu_custom_call" | custom-call | tf_op jit(solution)/shard_map/pallas_call | solution.py:373
  98.6 5.5 %shard_map.65 = bf16[16,256,1536]{2,1,0:T(8,128)(2,1)} custom-call(bf16[16,256,1536]{2,1,0:T(8,128)(2,1)S(1)} %get-tuple-element.11.xb, bf16[1536,1536]{1,0:T(8,128)(2,1)S(1)} %get-tuple-element.12.wo, bf16[8,512,128]{2,1,0:T(8,128)(2,1)S(1)} %get-tuple-element.13.kv_end, bf16[6,256,128]{2,1,0:T(8,128)(2,1)S(1)} %get-tuple-element.14.q_head, ...), custom_call_target="tpu_custom_call" | custom-call | tf_op jit(solution)/shard_map/pallas_call | solution.py:403

commit v7 on v6

--- a/solution.py
+++ b/solution.py
@@ -134,8 +134,8 @@
 
     w_copies[0].start()
     x_copy(0).start()
+    w_copies[1].start()
     w_copies[4].start()
-    w_copies[1].start()
     barrier = pltpu.get_barrier_semaphore()
     for other in (sib, par):
         pl.semaphore_signal(barrier, inc=1, device_id={"cp": other}, device_id_type=MESH)
@@ -226,11 +226,11 @@
 
     for copy in (w_copies[4], w_copies[0], x_copy(0)):
         copy.wait()
+    w_copies[1].wait()
     for b in range(1, 5):
         x_copy(b).start()
-    w_copies[1].wait()
+    pl.semaphore_wait(barrier, 2)
     make_kv(0)
-    pl.semaphore_wait(barrier, 2)
     send_row(0)
 
     def kv_step(i, _):

time: 104 us -> 105 us (level)
  no operation moved by 1% of the time
where the time goes in v7:
time: 105 us; the launch traced here: 104 us
  Pallas kernels  104 us (99%)
    pallas_call x1, Pallas kernels, local_block(): pl.pallas_call(main_kernel, out_shape=[pltpu.VMEM(x_loc.shape, bf16), plt...  98.6 us
    pallas_call x1, Pallas kernels, local_block(): pl.pallas_call(end_kernel, out_shape=jax.ShapeDtypeStruct(x_loc.shape, bf...  5.53 us

profile of v7, /device:TPU:0, one launch (start us, length us, event | category | flops | bytes accessed | tf_op | source)
XLA Modules:
  0.0 104.4 jit_solution(14250987994905319861)
XLA Ops:
  0.0 98.6 %shard_map.64 = (bf16[16,256,1536]{2,1,0:T(8,128)(2,1)S(1)}, bf16[1536,1536]{1,0:T(8,128)(2,1)S(1)}, bf16[8,512,128]{2,1,0:T(8,128)(2,1)S(1)}, bf16[6,256,128]{2...) custom-call(bf16[16,256,1536]{2,1,0:T(8,128)(2,1)} %x_hbm.1, s32[16,256]{1,0:T(8,128)} %pos_hbm.1, ...), custom_call_target="tpu_custom_call" | custom-call | tf_op jit(solution)/shard_map/pallas_call | solution.py:373
  98.7 5.5 %shard_map.65 = bf16[16,256,1536]{2,1,0:T(8,128)(2,1)} custom-call(bf16[16,256,1536]{2,1,0:T(8,128)(2,1)S(1)} %get-tuple-element.11.xb, bf16[1536,1536]{1,0:T(8,128)(2,1)S(1)} %get-tuple-element.12.wo, bf16[8,512,128]{2,1,0:T(8,128)(2,1)S(1)} %get-tuple-element.13.kv_end, bf16[6,256,128]{2,1,0:T(8,128)(2,1)S(1)} %get-tuple-element.14.q_head, ...), custom_call_target="tpu_custom_call" | custom-call | tf_op jit(solution)/shard_map/pallas_call | solution.py:403
